TPU v7x, 8 devices: a whole 2x2x1 slice. The times are simulated.
8 devices in a mesh: dp: 2 (over z, y), tp: 4 (over x, core).
Axes of the slice: x: 2, y: 2, z: 1, core: 2. Of those that a mesh axis runs over, the one named last changes fastest.
Arguments:
- hidden: bfloat16 [4, 512, 7168], P('dp', 'tp'), parts along dimension 0
- lengths: int32 [4], P('dp'), parts along dimension 0
- rope_cos: float32 [4, 512, 32], P('dp'), parts along dimension 0
- rope_sin: float32 [4, 512, 32], P('dp'), parts along dimension 0
- cache_lat: bfloat16 [4, 1024, 512], P('dp'), parts along dimension 0
- cache_pe: bfloat16 [4, 1024, 64], P('dp'), parts along dimension 0
- norm_in: float32 [7168], replicated
- w_dq: bfloat16 [7168, 1536], replicated
- norm_q: float32 [1536], replicated
- w_dkv: bfloat16 [7168, 576], replicated
- norm_kv: float32 [512], replicated
- w_uq: bfloat16 [1536, 128, 192], P(None, 'tp')
- w_uk: bfloat16 [512, 128, 128], P(None, 'tp')
- w_uv: bfloat16 [512, 128, 128], P(None, 'tp')
- w_out: bfloat16 [16384, 7168], P('tp')
Outputs:
- output 1: bfloat16 [4, 512, 7168], P('dp', 'tp'), parts along dimension 0
- output 2: bfloat16 [4, 1024, 512], P('dp'), parts along dimension 0
- output 3: bfloat16 [4, 1024, 64], P('dp'), parts along dimension 0
There are 2 independent parts. A program takes and returns all parts, laid end to end along the dimension named above; an argument that names none is the same for every part.
All inputs are finite; a program needn't handle non-finite values.
Results may differ from a plain program's by a relative error of at most 0.0138019.
Values are sent between devices in bfloat16 or wider.
A program may use at most 1 GiB of HBM per device.

v0:
```python
import functools

import jax
import jax.numpy as jnp
from jax import lax
from jax.experimental import pallas as pl
from jax.experimental.pallas import tpu as pltpu
from jax.sharding import PartitionSpec as P


F32 = jnp.float32
BF16 = jnp.bfloat16
NEG = -1e30
LOG2E = 1.4426950408889634
COL_TILE = 512
COL_CHUNKS = 2
HEADS_PER_STEP = 2


def rms_norm(values, gain_vec):
    inv_rms = lax.rsqrt(jnp.mean(values * values, axis=-1, keepdims=True) + 1e-6)
    return values * inv_rms * gain_vec


def apply_rope(values, cos_tab, sin_tab):
    half_dim = values.shape[-1] // 2
    lower_half = values[..., :half_dim]
    upper_half = values[..., half_dim:]
    return jnp.concatenate([lower_half * cos_tab - upper_half * sin_tab, upper_half * cos_tab + lower_half * sin_tab], axis=-1)


def attention_kernel(scal_ref, q_ref, k_old_ref, k_new_ref, v_old_ref, v_new_ref, r_ref, cos_ref, sin_ref, o_ref, *, scale):
    heads, _, m_rows = q_ref.shape
    nope = k_old_ref.shape[2]
    prefix = k_old_ref.shape[1]
    rope_half = cos_ref.shape[0]
    blk = m_rows
    factor = scale * LOG2E
    cos_tab = cos_ref[...]
    sin_tab = sin_ref[...]
    pad_row = lax.broadcasted_iota(jnp.int32, (nope - 2 * rope_half, m_rows), 0)
    ones_row = jnp.where(pad_row == 0, 1.0, 0.0).astype(BF16)
    half = m_rows // 2
    qlane = lax.broadcasted_iota(jnp.int32, (blk, m_rows), 1)
    krow = lax.broadcasted_iota(jnp.int32, (blk, m_rows), 0)
    q_blk0 = scal_ref[0]
    q_blk1 = scal_ref[1]
    base = scal_ref[2] * m_rows
    qpos = jnp.where(qlane < half, q_blk0 * half + qlane, q_blk1 * half + qlane - half) - base
    causal = krow <= qpos

    def body(new_blocks):
        for h in range(heads):
            low = q_ref[h, nope:nope + rope_half, :]
            high = q_ref[h, nope + rope_half:, :]
            q_cat = jnp.concatenate([
                q_ref[h, :nope, :].astype(BF16),
                (low * cos_tab - high * sin_tab).astype(BF16),
                (high * cos_tab + low * sin_tab).astype(BF16),
                ones_row], axis=0)
            scores = []
            for i in range(prefix // blk + new_blocks):
                start = i * blk
                if start < prefix:
                    k_part = k_old_ref[h, start:start + blk, :]
                else:
                    k_part = k_new_ref[h, start - prefix:start - prefix + blk, :]
                k_cat = jnp.concatenate([k_part, r_ref[start:start + blk, :]], axis=1)
                s = jnp.dot(k_cat, q_cat, preferred_element_type=F32)
                if i == prefix // blk + new_blocks - 1:
                    s = jnp.where(causal, s, NEG)
                scores.append(s)
            top = functools.reduce(jnp.maximum, scores)
            top = jnp.max(top, axis=0, keepdims=True)
            total = None
            out = None
            for i, s in enumerate(scores):
                start = i * blk
                e = jnp.exp2((s - top) * factor)
                part = jnp.sum(e, axis=0, keepdims=True)
                total = part if total is None else total + part
                if start < prefix:
                    v_part = v_old_ref[h, :, start:start + blk]
                else:
                    v_part = v_new_ref[h, :, start - prefix:start - prefix + blk]
                o_part = jnp.dot(v_part, e.astype(BF16), preferred_element_type=F32)
                out = o_part if out is None else out + o_part
            out = out * (1.0 / total)
            o_ref[:, h * nope:(h + 1) * nope] = out.T.astype(BF16)

    for c in range(v_new_ref.shape[2] // blk):
        @pl.when(scal_ref[2] == c)
        def _(c=c):
            body(c + 1)


def attention(scal, q, q_tile, k_old, k_new, v_old, v_new, r_cat, cos_tab, sin_tab, scale):
    n_heads, q_dim, _ = q.shape
    m_rows = cos_tab.shape[1]
    prefix, nope = k_old.shape[1:]
    n_new = k_new.shape[1]
    hb = HEADS_PER_STEP
    flops = 2 * n_heads * m_rows * (prefix + n_new) * (256 + 128)
    head_blk = lambda *shape: pl.BlockSpec((hb,) + shape, lambda g, s: (g, 0, 0))
    whole = lambda *shape: pl.BlockSpec(shape, lambda g, s: (0, 0))
    return pl.pallas_call(
        functools.partial(attention_kernel, scale=scale),
        out_shape=jax.ShapeDtypeStruct((m_rows, n_heads * nope), BF16),
        grid_spec=pltpu.PrefetchScalarGridSpec(
            num_scalar_prefetch=1,
            grid=(n_heads // hb,),
            in_specs=[
                pl.BlockSpec((hb, q_dim, m_rows), lambda g, s: (g, 0, q_tile)),
                head_blk(prefix, nope),
                head_blk(n_new, nope),
                head_blk(nope, prefix),
                head_blk(nope, n_new),
                whole(*r_cat.shape),
                whole(*cos_tab.shape),
                whole(*sin_tab.shape),
            ],
            out_specs=pl.BlockSpec((m_rows, hb * nope), lambda g, s: (0, g)),
        ),
        compiler_params=pltpu.CompilerParams(dimension_semantics=("arbitrary",)),
        cost_estimate=pl.CostEstimate(flops=flops, bytes_accessed=30_000_000, transcendentals=n_heads * m_rows * (prefix + n_new)),
        name="attention",
    )(scal, q, k_old, k_new, v_old, v_new, r_cat, cos_tab, sin_tab)


def out_proj_kernel(o_ref, w_ref, ya_ref, yb_ref):
    half = ya_ref.shape[0]
    prod = jnp.dot(o_ref[...], w_ref[...], preferred_element_type=F32)
    ya_ref[...] = prod[:half]
    yb_ref[...] = prod[half:]


def out_proj(o, w_out, first, count):
    m_rows, depth = o.shape
    half = m_rows // 2
    tiles = count // COL_TILE
    off = first // COL_TILE
    out = jax.ShapeDtypeStruct((half, count), F32)
    return pl.pallas_call(
        out_proj_kernel,
        out_shape=(out, out),
        grid=(tiles,),
        in_specs=[
            pl.BlockSpec((m_rows, depth), lambda j: (0, 0)),
            pl.BlockSpec((depth, COL_TILE), lambda j: (0, j + off)),
        ],
        out_specs=(pl.BlockSpec((half, COL_TILE), lambda j: (0, j)), pl.BlockSpec((half, COL_TILE), lambda j: (0, j))),
        compiler_params=pltpu.CompilerParams(dimension_semantics=("arbitrary",)),
        cost_estimate=pl.CostEstimate(flops=2 * m_rows * depth * count, bytes_accessed=depth * count * 2 + m_rows * count * 4, transcendentals=0),
        name="out_proj",
    )(o, w_out)


def solution(mesh):
    tp = mesh.shape["tp"]
    to_partner = [(i, i ^ 1) for i in range(tp)]
    to_chip = [(i, i ^ 2) for i in range(tp)]

    def partner(value):
        return lax.ppermute(value, "tp", to_partner)

    def other_chip(value):
        return lax.ppermute(value, "tp", to_chip)

    def step(hidden, lengths, rope_cos, rope_sin, cache_lat, cache_pe, norm_in, w_dq, norm_q, w_dkv, norm_kv, w_uq, w_uk, w_uv, w_out):
        me = lax.axis_index("tp")
        n_seq, n_tok, model_dim = hidden.shape
        kv_rank, _, nope = w_uk.shape
        rope_dim = cache_pe.shape[2]
        n_new = rope_cos.shape[1]
        prefix = cache_lat.shape[1] - n_new
        q_rank = w_dq.shape[1]
        scale = (nope + rope_dim) ** -0.5

        normed = rms_norm(hidden.astype(F32), norm_in).astype(BF16).reshape(n_seq * n_tok, model_dim)
        kv_proj = jnp.dot(normed, w_dkv, preferred_element_type=F32).reshape(n_seq, n_tok, kv_rank + rope_dim)
        my_cos = lax.dynamic_slice_in_dim(rope_cos, me * n_tok, n_tok, axis=1)
        my_sin = lax.dynamic_slice_in_dim(rope_sin, me * n_tok, n_tok, axis=1)
        my_lat = rms_norm(kv_proj[..., :kv_rank], norm_kv).astype(BF16)
        my_pe = apply_rope(kv_proj[..., kv_rank:], my_cos, my_sin).astype(BF16)
        my_kv = jnp.concatenate([my_lat, my_pe], axis=-1)
        my_q = rms_norm(jnp.dot(normed, w_dq, preferred_element_type=F32), norm_q).astype(BF16).reshape(n_seq, n_tok, q_rank)

        def gather(value):
            far = other_chip(value)
            near = partner(value)
            return [value, near, far, partner(far)]

        kv_rel = jnp.stack(gather(my_kv))
        kv_true = jnp.concatenate([lax.dynamic_index_in_dim(kv_rel, me ^ j, keepdims=False) for j in range(tp)], axis=1)
        lat_new = kv_true[..., :kv_rank]
        pe_new = kv_true[..., kv_rank:]
        q_rel = [gather(my_q[b]) for b in range(n_seq)]

        def project(lat):
            keys = jnp.einsum("sc,chd->hsd", lat, w_uk, preferred_element_type=F32).astype(BF16)
            values = jnp.einsum("chv,sc->hvs", w_uv, lat, preferred_element_type=F32).astype(BF16)
            return keys, values

        row = jnp.arange(prefix)
        alive = row[None, :] < lengths[:, None]
        old_lat = jnp.where(alive[..., None], cache_lat[:, :prefix], 0)
        old_pe = jnp.where(alive[..., None], cache_pe[:, :prefix], 0)
        kv_old = [project(old_lat[b]) for b in range(n_seq)]
        kv_new = [project(lat_new[b]) for b in range(n_seq)]
        bias = jnp.where(alive, 0.0, NEG).astype(BF16)[..., None]
        pad_old = jnp.zeros((n_seq, prefix, nope - rope_dim - 1), BF16)
        pad_new = jnp.zeros((n_seq, n_new, nope - rope_dim), BF16)
        r_cat = jnp.concatenate([
            jnp.concatenate([old_pe, bias, pad_old], axis=-1),
            jnp.concatenate([pe_new, pad_new], axis=-1)], axis=1)

        def queries(q_lat):
            return jnp.einsum("qhd,tq->hdt", w_uq, q_lat, preferred_element_type=F32)

        def attend(rel, b, q, q_tile):
            blocks = (me ^ rel, me ^ (rel + 1))
            scal = jnp.stack([blocks[0], blocks[1], blocks[0] // 2]).astype(jnp.int32)
            cut = lambda tab: jnp.concatenate([lax.dynamic_slice_in_dim(tab[b], k * n_tok, n_tok, axis=0) for k in blocks], axis=0).T
            return attention(scal, q, q_tile, kv_old[b][0], kv_new[b][0], kv_old[b][1], kv_new[b][1], r_cat[b], cut(rope_cos), cut(rope_sin), scale)

        def after(value, *deps):
            return lax.optimization_barrier((value,) + deps)[0]

        width = model_dim // COL_CHUNKS
        arrived = [[None] * COL_CHUNKS for _ in range(n_seq)]
        pending = []

        def send_one():
            b, j, near_part, came = pending.pop(0)
            summed = near_part + came
            arrived[b][j] = other_chip(summed)
            return summed

        near_part = None
        for b in range(n_seq):
            q_lat = jnp.concatenate(q_rel[b][2:], axis=0)
            if near_part is not None:
                q_lat = after(q_lat, near_part)
            q = queries(q_lat)
            if pending:
                q = after(q, send_one())
            o = attend(2, b, q, 0)
            for j in range(COL_CHUNKS):
                if len(pending) > 1 - (j == 0):
                    o = after(o, send_one())
                near_part, far_part = out_proj(o, w_out, j * width, width)
                pending.append((b, j, near_part, partner(far_part)))
        q_lat = jnp.concatenate([q_rel[b][k] for b in range(n_seq) for k in (0, 1)], axis=0)
        q_lat = after(q_lat, near_part)
        q_own = queries(q_lat)
        while pending:
            q_own = after(q_own, send_one())
        result = []
        for b in range(n_seq):
            o = attend(0, b, q_own, b)
            own_part, partner_part = out_proj(o, w_out, 0, model_dim)
            base = own_part + partner(partner_part) + hidden[b].astype(F32)
            result.append((base + jnp.concatenate(arrived[b], axis=1)).astype(BF16))
        out = jnp.stack(result)
        lat_all = jnp.stack([lax.dynamic_update_slice(cache_lat[b], lat_new[b], (lengths[b], 0)) for b in range(n_seq)])
        pe_all = jnp.stack([lax.dynamic_update_slice(cache_pe[b], pe_new[b], (lengths[b], 0)) for b in range(n_seq)])
        return out, lat_all, pe_all

    spec_tok = P("dp", "tp", None)
    spec_len = P("dp")
    spec_seq = P("dp", None, None)
    spec_vec = P(None)
    spec_mat = P(None, None)
    spec_head = P(None, "tp", None)
    spec_rows = P("tp", None)
    in_specs = (spec_tok, spec_len, spec_seq, spec_seq, spec_seq, spec_seq, spec_vec, spec_mat, spec_vec, spec_mat, spec_vec, spec_head, spec_head, spec_head, spec_rows)
    return jax.shard_map(step, mesh=mesh, in_specs=in_specs, out_specs=(spec_tok, spec_seq, spec_seq), check_vma=False)
```

profile of v0, /device:TPU:0, one launch (start us, length us, event | category | flops | bytes accessed | tf_op | source)
XLA Modules:
  0.0 495.5 jit_solution(10153869360978499881)
XLA Ops:
  0.6 3.0 fusion.2
  3.8 1.8 fusion.4
  5.6 6.2 %fusion = f32[2,128,576]{1,2,0:T(8,128)S(1)} fusion(bf16[2,128,7168]{2,1,0:T(8,128)(2,1)S(1)} %fusion.4, bf16[7168,576]{0,1:T(8,128)(2,1)} %param.24), kind=kOutput, calls=%fused_computation.2 | convolution fusion | flops 2113929216 | bytes 12517376 | tf_op jit(solution)/shard_map/dot_general | solution.py:180
  13.7 3.3 collective-permute-start.7
  17.0 11.6 %multiply_reduce_fusion = (f32[256]{0:T(256)S(1)}, f32[256,1536]{1,0:T(8,128)S(1)}) fusion(bf16[256,7168]{1,0:T(8,128)(2,1)} %bitcast.145, bf16[7168,1536]{1,0:T(8,128)(2,1)} %param.22), kind=kOutput, calls=%fused_computation.43 | convolution fusion | flops 5637931008 | bytes 27264000 | tf_op jit(solution)/shard_map/dot_general | solution.py:186
  29.4 1.7 collective-permute-start.2
  32.4 8.0 %convert_bitcast_fusion.5.v_old_ref = bf16[32,128,512]{2,1,0:T(8,128)(2,1)} fusion(bf16[512,32,128]{2,1,0:T(8,128)(2,1)} %param.28, bf16[2,512,512]{2,1,0:T(8,128)(2,1)S(1)} %slice_select_fusion), kind=kOutput, calls=%fused_computation.12 | convolution fusion | flops 2149580800 | bytes 8912896 | tf_op jit(solution)/shard_map/chv,sc->hvs/dot_general | solution.py:201
  40.3 6.1 %convert_bitcast_fusion.1.v_old_ref = bf16[32,128,512]{2,1,0:T(8,128)(2,1)} fusion(bf16[512,32,128]{2,1,0:T(8,128)(2,1)S(1)} %copy-done.28, bf16[2,512,512]{2,1,0:T(8,128)(2,1)S(1)} %slice_select_fusion), kind=kOutput, calls=%fused_computation.8 | convolution fusion | flops 2149580800 | bytes 8912896 | tf_op jit(solution)/shard_map/chv,sc->hvs/dot_general | solution.py:201
  46.4 4.5 convert_bitcast_fusion.7.k_old_ref
  50.9 4.8 convert_bitcast_fusion.3.k_old_ref
  66.6 8.4 %convert_bitcast_fusion.4.v_new_ref = bf16[32,128,512]{2,1,0:T(8,128)(2,1)} fusion(bf16[512,32,128]{2,1,0:T(8,128)(2,1)} %param.28, bf16[2,512,576]{2,1,0:T(8,128)(2,1)S(1)} %pad_maximum_fusion.3), kind=kOutput, calls=%fused_computation.11 | convolution fusion | flops 2149580800 | bytes 8912896 | tf_op jit(solution)/shard_map/chv,sc->hvs/dot_general | solution.py:201
  75.1 4.5 convert_bitcast_fusion.6.k_new_ref
  79.7 6.4 %convert_bitcast_fusion.v_new_ref = bf16[32,128,512]{2,1,0:T(8,128)(2,1)} fusion(bf16[512,32,128]{2,1,0:T(8,128)(2,1)S(1)} %copy-done.29, bf16[2,512,576]{2,1,0:T(8,128)(2,1)S(1)} %pad_maximum_fusion.3), kind=kOutput, calls=%fused_computation.7 | convolution fusion | flops 2149580800 | bytes 8912896 | tf_op jit(solution)/shard_map/chv,sc->hvs/dot_general | solution.py:201
  87.2 7.1 %convert_bitcast_fusion.2.k_new_ref = bf16[32,512,128]{2,1,0:T(8,128)(2,1)} fusion(bf16[512,32,128]{2,1,0:T(8,128)(2,1)} %param.27, bf16[2,512,576]{2,1,0:T(8,128)(2,1)S(1)} %pad_maximum_fusion.3), kind=kOutput, calls=%fused_computation.9 | convolution fusion | flops 2149580800 | bytes 8912896 | tf_op jit(solution)/shard_map/sc,chd->hsd/dot_general | solution.py:200
  94.3 8.3 %fusion.42 = f32[256,6144]{0,1} fusion(bf16[1536,6144]{0,1:T(8,128)(2,1)S(1)} %bitcast.159, bf16[128,1536]{1,0:T(8,128)(2,1)} %collective-permute-done.5, bf16[128,1536]{1,0:T(8,128)(2,1)} %collective-permute-done.4), kind=kOutput, calls=%fused_computation.50 | convolution fusion | flops 4833411072 | bytes 25952256
  102.6 24.3 %attention.4.o_ref = bf16[256,4096]{1,0:T(8,128)(2,1)} custom-call(s32[3]{0:T(128)} %pad_add_fusion.1.scal_ref, f32[32,192,256]{2,1,0:T(8,128)} %bitcast.144, bf16[32,512,128]{2,1,0:T(8,128)(2,1)} %convert_bitcast_fusion.7.k_old_ref, bf16[32,512,128]{2,1,0:T(8,128)(2,1)} %convert_bitcast_fusion.6.k_new_ref, ...), custom_call_target="tpu_custom_call" | custom-call | flops 6442450944 | bytes 30000000 | tf_op jit(solution)/shard_map/attention/pallas_call | solution.py:106
  126.9 16.1 %out_proj.7 = (f32[128,3584]{1,0:T(8,128)}, f32[128,3584]{1,0:T(8,128)}) custom-call(bf16[256,4096]{1,0:T(8,128)(2,1)} %attention.4.o_ref, bf16[4096,7168]{1,0:T(8,128)(2,1)} %w_ref.11), custom_call_target="tpu_custom_call" | custom-call | flops 7516192768 | bytes 33030144 | tf_op jit(solution)/shard_map/out_proj/pallas_call | solution.py:143
  143.0 16.1 %out_proj.6 = (f32[128,3584]{1,0:T(8,128)}, f32[128,3584]{1,0:T(8,128)}) custom-call(bf16[256,4096]{1,0:T(8,128)(2,1)} %attention.4.o_ref, bf16[4096,7168]{1,0:T(8,128)(2,1)} %w_ref.11), custom_call_target="tpu_custom_call" | custom-call | flops 7516192768 | bytes 33030144 | tf_op jit(solution)/shard_map/out_proj/pallas_call | solution.py:143
  160.8 11.7 %fusion.64 = f32[256,6144]{0,1} fusion(bf16[256,1536]{1,0:T(8,128)(2,1)S(1)} %pad_maximum_fusion.5, bf16[1536,6144]{0,1:T(8,128)(2,1)} %bitcast.155), kind=kOutput, calls=%fused_computation.121 | convolution fusion | flops 4831838208 | bytes 25952256
  172.5 1.4 add.123
  173.9 24.5 %attention.5.o_ref = bf16[256,4096]{1,0:T(8,128)(2,1)} custom-call(s32[3]{0:T(128)} %pad_add_fusion.1.scal_ref, f32[32,192,256]{2,1,0:T(8,128)} %bitcast.143, bf16[32,512,128]{2,1,0:T(8,128)(2,1)} %convert_bitcast_fusion.3.k_old_ref, bf16[32,512,128]{2,1,0:T(8,128)(2,1)} %convert_bitcast_fusion.2.k_new_ref, ...), custom_call_target="tpu_custom_call" | custom-call | flops 6442450944 | bytes 30000000 | tf_op jit(solution)/shard_map/attention/pallas_call | solution.py:106
  198.4 2.9 add.124
  201.4 16.1 %out_proj.8 = (f32[128,3584]{1,0:T(8,128)}, f32[128,3584]{1,0:T(8,128)}) custom-call(bf16[256,4096]{1,0:T(8,128)(2,1)} %attention.5.o_ref, bf16[4096,7168]{1,0:T(8,128)(2,1)} %w_ref.11), custom_call_target="tpu_custom_call" | custom-call | flops 7516192768 | bytes 33030144 | tf_op jit(solution)/shard_map/out_proj/pallas_call | solution.py:143
  217.5 16.1 %out_proj.9 = (f32[128,3584]{1,0:T(8,128)}, f32[128,3584]{1,0:T(8,128)}) custom-call(bf16[256,4096]{1,0:T(8,128)(2,1)} %attention.5.o_ref, bf16[4096,7168]{1,0:T(8,128)(2,1)} %w_ref.11), custom_call_target="tpu_custom_call" | custom-call | flops 7516192768 | bytes 33030144 | tf_op jit(solution)/shard_map/out_proj/pallas_call | solution.py:143
  234.0 1.2 pad_maximum_fusion.2
  235.3 16.8 %fusion.65 = f32[512,6144]{0,1} fusion(bf16[512,1536]{1,0:T(8,128)(2,1)S(1)} %pad_maximum_fusion.2, bf16[1536,6144]{0,1:T(8,128)(2,1)} %bitcast.156), kind=kOutput, calls=%fused_computation.122 | convolution fusion | flops 9663676416 | bytes 33030144
  252.1 1.4 add.125
  254.3 1.5 add.126
  255.8 23.2 %attention.7.o_ref = bf16[256,4096]{1,0:T(8,128)(2,1)} custom-call(s32[3]{0:T(128)} %pad_add_fusion.scal_ref, f32[32,192,512]{2,1,0:T(8,128)} %bitcast.141, bf16[32,512,128]{2,1,0:T(8,128)(2,1)} %convert_bitcast_fusion.3.k_old_ref, bf16[32,512,128]{2,1,0:T(8,128)(2,1)} %convert_bitcast_fusion.2.k_new_ref, ...), custom_call_target="tpu_custom_call" | custom-call | flops 6442450944 | bytes 30000000 | tf_op jit(solution)/shard_map/attention/pallas_call | solution.py:106
  279.0 29.1 %out_proj.11 = (f32[128,7168]{1,0:T(8,128)}, f32[128,7168]{1,0:T(8,128)}) custom-call(bf16[256,4096]{1,0:T(8,128)(2,1)} %attention.7.o_ref, bf16[4096,7168]{1,0:T(8,128)(2,1)} %w_ref.11), custom_call_target="tpu_custom_call" | custom-call | flops 15032385536 | bytes 66060288 | tf_op jit(solution)/shard_map/out_proj/pallas_call | solution.py:143
  308.2 23.4 %attention.6.o_ref = bf16[256,4096]{1,0:T(8,128)(2,1)} custom-call(s32[3]{0:T(128)} %pad_add_fusion.scal_ref, f32[32,192,512]{2,1,0:T(8,128)} %bitcast.142, bf16[32,512,128]{2,1,0:T(8,128)(2,1)} %convert_bitcast_fusion.7.k_old_ref, bf16[32,512,128]{2,1,0:T(8,128)(2,1)} %convert_bitcast_fusion.6.k_new_ref, ...), custom_call_target="tpu_custom_call" | custom-call | flops 6442450944 | bytes 30000000 | tf_op jit(solution)/shard_map/attention/pallas_call | solution.py:106
  331.7 29.3 %out_proj.10 = (f32[128,7168]{1,0:T(8,128)}, f32[128,7168]{1,0:T(8,128)}) custom-call(bf16[256,4096]{1,0:T(8,128)(2,1)} %attention.6.o_ref, bf16[4096,7168]{1,0:T(8,128)(2,1)} %w_ref.11), custom_call_target="tpu_custom_call" | custom-call | flops 15032385536 | bytes 66060288 | tf_op jit(solution)/shard_map/out_proj/pallas_call | solution.py:143
  361.4 4.1 collective-permute-start.15
  365.5 2.0 collective-permute-start.17
  372.0 1.8 fusion.60
  373.8 1.5 fusion.57
  376.0 1.6 copy.35
  378.4 1.8 dynamic_update_slice.18
  381.3 4.0 dynamic_update_slice.16
  385.3 1.6 dynamic_update_slice.19
  386.9 3.8 dynamic_update_slice.17
  390.7 1.8 pad_maximum_fusion.7
  392.5 1.5 pad_maximum_fusion.1
  394.0 12.7 %collective-permute-done.15 = f32[128,3584]{1,0:T(8,128)} collective-permute-done((f32[128,3584]{1,0:T(8,128)}, f32[128,3584]{1,0:T(8,128)}, u32[]{:S(2)}, u32[]{:S(2)}) %collective-permute-start.15) | collective-permute-done | bytes 1835040 | tf_op jit(solution)/shard_map/ppermute | solution.py:167
  406.7 39.3 %collective-permute-done.18 = f32[128,3584]{1,0:T(8,128)} collective-permute-done((f32[128,3584]{1,0:T(8,128)}, f32[128,3584]{1,0:T(8,128)}, u32[]{:S(2)}, u32[]{:S(2)}) %collective-permute-start.18) | collective-permute-done | bytes 1835040 | tf_op jit(solution)/shard_map/ppermute | solution.py:167
  446.0 38.7 %collective-permute-done.17 = f32[128,3584]{1,0:T(8,128)} collective-permute-done((f32[128,3584]{1,0:T(8,128)}, f32[128,3584]{1,0:T(8,128)}, u32[]{:S(2)}, u32[]{:S(2)}) %collective-permute-start.17) | collective-permute-done | bytes 1835040 | tf_op jit(solution)/shard_map/ppermute | solution.py:167
  484.7 8.4 %fusion.40 = (bf16[1,128,7168]{2,1,0:T(8,128)(2,1)S(1)}, bf16[1,128,7168]{2,1,0:T(8,128)(2,1)S(1)}) fusion(f32[128,3584]{1,0:T(8,128)} %collective-permute-done.15, f32[128,3584]{1,0:T(8,128)} %collective-permute-done.14, f32[128,7168]{1,0:T(8,128)} %get-tuple-element.35, f32[128,7168]{1,0:T(8,128)} %collective-permute-done.13, ...), kind=kLoop, calls=%fused_computation.40 | loop fusion | flops 11010048 | bytes 29360128 | tf_op jit(solution)/shard_map/stack | solution.py:264
  493.1 2.2 pad_maximum_fusion
  (153 shorter events, 22.5 us)
Async XLA Ops:
  5.6 6.2 %copy-start.8 = (bf16[2,128,7168]{2,1,0:T(8,128)(2,1)}, bf16[2,128,7168]{2,1,0:T(8,128)(2,1)S(1)}, u32[]{:S(2)}) copy-start(bf16[2,128,7168]{2,1,0:T(8,128)(2,1)S(1)} %fusion.4) | copy-start | bytes 11010052
  5.6 6.3 %copy-start.27 = (f32[512]{0:T(512)S(1)}, f32[512]{0:T(512)}, u32[]{:S(2)}) copy-start(f32[512]{0:T(512)} %param.25) | copy-start | bytes 6148
  5.6 6.5 %copy-start.23 = (f32[2,512,32]{1,2,0:T(8,128)S(1)}, f32[2,512,32]{1,2,0:T(8,128)}, u32[]{:S(2)}) copy-start(f32[2,512,32]{1,2,0:T(8,128)} %param.18) | copy-start | bytes 393220
  13.7 48.1 %collective-permute-start.7 = (bf16[2,128,576]{1,2,0:T(8,128)(2,1)}, bf16[2,128,576]{1,2,0:T(8,128)(2,1)}, u32[]{:S(2)}, u32[]{:S(2)}) collective-permute-start(bf16[2,128,576]{1,2,0:T(8,128)(2,1)} %get-tuple-element.58), channel_id=1, source_target_pairs={{0,2},{1,3},{2,0},{3,1},{4,6},{5,7},{6,4},{7,5}} | collective-permute-start | bytes 884744 | tf_op jit(solution)/shard_map/ppermute | solution.py:167
  17.0 46.3 %collective-permute-start.6 = (bf16[2,128,576]{1,2,0:T(8,128)(2,1)}, bf16[2,128,576]{1,2,0:T(8,128)(2,1)}, u32[]{:S(2)}, u32[]{:S(2)}) collective-permute-start(bf16[2,128,576]{1,2,0:T(8,128)(2,1)} %get-tuple-element.58), channel_id=1, source_target_pairs={{0,1},{1,0},{2,3},{3,2},{4,5},{5,4},{6,7},{7,6}} | collective-permute-start | bytes 884744 | tf_op jit(solution)/shard_map/ppermute | solution.py:164
  17.0 11.6 %copy-start.24 = (f32[1536]{0:T(1024)S(1)}, f32[1536]{0:T(1024)}, u32[]{:S(2)}) copy-start(f32[1536]{0:T(1024)} %param.23) | copy-start | bytes 18436
  28.9 34.9 %collective-permute-start.4 = (bf16[128,1536]{1,0:T(8,128)(2,1)S(1)}, bf16[128,1536]{1,0:T(8,128)(2,1)}, u32[]{:S(2)}, u32[]{:S(2)}) collective-permute-start(bf16[128,1536]{1,0:T(8,128)(2,1)S(1)} %get-tuple-element.53), channel_id=1, source_target_pairs={{0,2},{1,3},{2,0},{3,1},{4,6},{5,7},{6,4},{7,5}} | collective-permute-start | bytes 1179656 | tf_op jit(solution)/shard_map/ppermute | solution.py:167
  28.9 205.1 %collective-permute-start = (bf16[128,1536]{1,0:T(8,128)(2,1)S(1)}, bf16[128,1536]{1,0:T(8,128)(2,1)}, u32[]{:S(2)}, u32[]{:S(2)}) collective-permute-start(bf16[128,1536]{1,0:T(8,128)(2,1)S(1)} %get-tuple-element.53), channel_id=1, source_target_pairs={{0,1},{1,0},{2,3},{3,2},{4,5},{5,4},{6,7},{7,6}} | collective-permute-start | bytes 1179656 | tf_op jit(solution)/shard_map/ppermute | solution.py:164
  29.4 34.4 %collective-permute-start.2 = (bf16[128,1536]{1,0:T(8,128)(2,1)S(1)}, bf16[128,1536]{1,0:T(8,128)(2,1)}, u32[]{:S(2)}, u32[]{:S(2)}) collective-permute-start(bf16[128,1536]{1,0:T(8,128)(2,1)S(1)} %get-tuple-element.54), channel_id=1, source_target_pairs={{0,2},{1,3},{2,0},{3,1},{4,6},{5,7},{6,4},{7,5}} | collective-permute-start | bytes 1179656 | tf_op jit(solution)/shard_map/ppermute | solution.py:167
  32.4 8.0 %copy-start.28 = (bf16[512,32,128]{2,1,0:T(8,128)(2,1)S(1)}, bf16[512,32,128]{2,1,0:T(8,128)(2,1)}, u32[]{:S(2)}) copy-start(bf16[512,32,128]{2,1,0:T(8,128)(2,1)} %param.28) | copy-start | bytes 12582916
  40.3 6.1 %copy-start.30 = (bf16[512,32,128]{2,1,0:T(8,128)(2,1)S(1)}, bf16[512,32,128]{2,1,0:T(8,128)(2,1)}, u32[]{:S(2)}) copy-start(bf16[512,32,128]{2,1,0:T(8,128)(2,1)} %param.27) | copy-start | bytes 12582916
  50.9 10.5 %slice-start = ((bf16[2,1024,64]{1,2,0:T(8,128)(2,1)}), bf16[2,512,64]{1,2,0:T(8,128)(2,1)S(1)}, s32[]{:S(2)}) async-start(bf16[2,1024,64]{1,2,0:T(8,128)(2,1)} %param.20), calls=%async_computation | async-start | bytes 262144 | tf_op jit(solution)/shard_map/slice | solution.py:207
  61.8 2.5 collective-permute-start.8
  63.3 170.8 %collective-permute-start.1 = (bf16[128,1536]{1,0:T(8,128)(2,1)S(1)}, bf16[128,1536]{1,0:T(8,128)(2,1)}, u32[]{:S(2)}, u32[]{:S(2)}) collective-permute-start(bf16[128,1536]{1,0:T(8,128)(2,1)S(1)} %get-tuple-element.54), channel_id=1, source_target_pairs={{0,1},{1,0},{2,3},{3,2},{4,5},{5,4},{6,7},{7,6}} | collective-permute-start | bytes 1179656 | tf_op jit(solution)/shard_map/ppermute | solution.py:164
  63.8 30.5 %collective-permute-start.5 = (bf16[128,1536]{1,0:T(8,128)(2,1)}, bf16[128,1536]{1,0:T(8,128)(2,1)}, u32[]{:S(2)}, u32[]{:S(2)}) collective-permute-start(bf16[128,1536]{1,0:T(8,128)(2,1)} %collective-permute-done.4), channel_id=1, source_target_pairs={{0,1},{1,0},{2,3},{3,2},{4,5},{5,4},{6,7},{7,6}} | collective-permute-start | bytes 1179656 | tf_op jit(solution)/shard_map/ppermute | solution.py:164
  63.8 95.3 %collective-permute-start.3 = (bf16[128,1536]{1,0:T(8,128)(2,1)}, bf16[128,1536]{1,0:T(8,128)(2,1)}, u32[]{:S(2)}, u32[]{:S(2)}) collective-permute-start(bf16[128,1536]{1,0:T(8,128)(2,1)} %collective-permute-done.2), channel_id=1, source_target_pairs={{0,1},{1,0},{2,3},{3,2},{4,5},{5,4},{6,7},{7,6}} | collective-permute-start | bytes 1179656 | tf_op jit(solution)/shard_map/ppermute | solution.py:164
  65.8 9.3 %copy-start.9 = (bf16[1,2,128,576]{3,2,1,0:T(8,128)(2,1)}, bf16[1,2,128,576]{3,2,1,0:T(8,128)(2,1)S(1)}, u32[]{:S(2)}) copy-start(bf16[1,2,128,576]{3,2,1,0:T(8,128)(2,1)S(1)} %copy.19) | copy-start | bytes 884740
  66.0 9.1 %copy-start.11 = (bf16[1,2,128,576]{3,2,1,0:T(8,128)(2,1)}, bf16[1,2,128,576]{3,2,1,0:T(8,128)(2,1)S(1)}, u32[]{:S(2)}) copy-start(bf16[1,2,128,576]{3,2,1,0:T(8,128)(2,1)S(1)} %copy.20) | copy-start | bytes 884740
  66.2 8.8 %copy-start.13 = (bf16[1,2,128,576]{3,2,1,0:T(8,128)(2,1)}, bf16[1,2,128,576]{3,2,1,0:T(8,128)(2,1)S(1)}, u32[]{:S(2)}) copy-start(bf16[1,2,128,576]{3,2,1,0:T(8,128)(2,1)S(1)} %copy.21) | copy-start | bytes 884740
  66.5 8.6 %copy-start.15 = (bf16[1,2,128,576]{3,2,1,0:T(8,128)(2,1)}, bf16[1,2,128,576]{3,2,1,0:T(8,128)(2,1)S(1)}, u32[]{:S(2)}) copy-start(bf16[1,2,128,576]{3,2,1,0:T(8,128)(2,1)S(1)} %copy.22) | copy-start | bytes 884740
  66.6 20.6 %copy-start.2 = (bf16[2,512,576]{2,1,0:T(8,128)(2,1)}, bf16[2,512,576]{2,1,0:T(8,128)(2,1)S(1)}, u32[]{:S(2)}) copy-start(bf16[2,512,576]{2,1,0:T(8,128)(2,1)S(1)} %pad_maximum_fusion.3) | copy-start | bytes 3538948
  66.6 8.5 %copy-start.31 = (bf16[512,32,128]{2,1,0:T(8,128)(2,1)S(1)}, bf16[512,32,128]{2,1,0:T(8,128)(2,1)}, u32[]{:S(2)}) copy-start(bf16[512,32,128]{2,1,0:T(8,128)(2,1)} %param.27) | copy-start | bytes 12582916
  66.6 13.0 %copy-start.29 = (bf16[512,32,128]{2,1,0:T(8,128)(2,1)S(1)}, bf16[512,32,128]{2,1,0:T(8,128)(2,1)}, u32[]{:S(2)}) copy-start(bf16[512,32,128]{2,1,0:T(8,128)(2,1)} %param.28) | copy-start | bytes 12582916
  75.1 19.1 %slice-start.1 = ((s8[18874368]{0:T(1024)(128)(4,1)}), s8[4194304]{0:T(1024)(128)(4,1)S(1)}, s32[]{:S(2)}) async-start(s8[18874368]{0:T(1024)(128)(4,1)} %bitcast.157), calls=%async_computation.1 | async-start | bytes 8388608
  75.1 19.1 %slice-start.2 = ((s8[18874368]{0:T(1024)(128)(4,1)}), s8[4194304]{0:T(1024)(128)(4,1)S(1)}, s32[]{:S(2)}) async-start(s8[18874368]{0:T(1024)(128)(4,1)} %bitcast.157), calls=%async_computation.2 | async-start | bytes 8388608
  79.6 6.5 %copy-start.21 = (bf16[2,512,64]{2,1,0:T(8,128)(2,1)S(1)}, bf16[2,512,64]{2,1,0:T(8,128)(2,1)}, u32[]{:S(2)}) copy-start(bf16[2,512,64]{2,1,0:T(8,128)(2,1)} %broadcast_select_fusion) | copy-start | bytes 393220
  79.6 14.6 %slice-start.3 = ((s8[18874368]{0:T(1024)(128)(4,1)}), s8[4194304]{0:T(1024)(128)(4,1)S(1)}, s32[]{:S(2)}) async-start(s8[18874368]{0:T(1024)(128)(4,1)} %bitcast.157), calls=%async_computation.3 | async-start | bytes 8388608
  79.6 14.6 %slice-start.4 = ((s8[18874368]{0:T(1024)(128)(4,1)}), s8[4194304]{0:T(1024)(128)(4,1)S(1)}, s32[]{:S(2)}) async-start(s8[18874368]{0:T(1024)(128)(4,1)} %bitcast.157), calls=%async_computation.4 | async-start | bytes 8388608
  87.2 7.1 %slice-start.5 = ((s8[18874368]{0:T(1024)(128)(4,1)}), s8[2097152]{0:T(1024)(128)(4,1)S(1)}, s32[]{:S(2)}) async-start(s8[18874368]{0:T(1024)(128)(4,1)} %bitcast.157), calls=%async_computation.5 | async-start | bytes 4194304
  143.0 29.5 %collective-permute-start.9 = (f32[128,3584]{1,0:T(8,128)}, f32[128,3584]{1,0:T(8,128)S(1)}, u32[]{:S(2)}, u32[]{:S(2)}) collective-permute-start(f32[128,3584]{1,0:T(8,128)} %get-tuple-element.24), channel_id=1, source_target_pairs={{0,1},{1,0},{2,3},{3,2},{4,5},{5,4},{6,7},{7,6}} | collective-permute-start | bytes 5505032 | tf_op jit(solution)/shard_map/ppermute | solution.py:164
  160.3 12.2 %copy-start.20 = (f32[128,3584]{1,0:T(8,128)S(1)}, f32[128,3584]{1,0:T(8,128)}, u32[]{:S(2)}) copy-start(f32[128,3584]{1,0:T(8,128)} %get-tuple-element.23) | copy-start | bytes 5505028
  160.3 38.2 %collective-permute-start.10 = (f32[128,3584]{1,0:T(8,128)}, f32[128,3584]{1,0:T(8,128)}, u32[]{:S(2)}, u32[]{:S(2)}) collective-permute-start(f32[128,3584]{1,0:T(8,128)} %get-tuple-element.26), channel_id=1, source_target_pairs={{0,1},{1,0},{2,3},{3,2},{4,5},{5,4},{6,7},{7,6}} | collective-permute-start | bytes 5505032 | tf_op jit(solution)/shard_map/ppermute | solution.py:164
  173.9 24.5 %copy-start.18 = (f32[128,3584]{1,0:T(8,128)S(1)}, f32[128,3584]{1,0:T(8,128)}, u32[]{:S(2)}) copy-start(f32[128,3584]{1,0:T(8,128)} %get-tuple-element.21) | copy-start | bytes 5505028
  217.4 36.1 %collective-permute-start.12 = (f32[128,3584]{1,0:T(8,128)}, f32[128,3584]{1,0:T(8,128)S(1)}, u32[]{:S(2)}, u32[]{:S(2)}) collective-permute-start(f32[128,3584]{1,0:T(8,128)} %get-tuple-element.33), channel_id=1, source_target_pairs={{0,1},{1,0},{2,3},{3,2},{4,5},{5,4},{6,7},{7,6}} | collective-permute-start | bytes 5505032 | tf_op jit(solution)/shard_map/ppermute | solution.py:164
  233.6 18.5 %collective-permute-start.11 = (f32[128,3584]{1,0:T(8,128)}, f32[128,3584]{1,0:T(8,128)S(1)}, u32[]{:S(2)}, u32[]{:S(2)}) collective-permute-start(f32[128,3584]{1,0:T(8,128)} %get-tuple-element.31), channel_id=1, source_target_pairs={{0,1},{1,0},{2,3},{3,2},{4,5},{5,4},{6,7},{7,6}} | collective-permute-start | bytes 5505032 | tf_op jit(solution)/shard_map/ppermute | solution.py:164
  235.3 130.3 %collective-permute-start.14 = (f32[128,3584]{1,0:T(8,128)}, f32[128,3584]{1,0:T(8,128)}, u32[]{:S(2)}, u32[]{:S(2)}) collective-permute-start(f32[128,3584]{1,0:T(8,128)} %add.123), channel_id=1, source_target_pairs={{0,2},{1,3},{2,0},{3,1},{4,6},{5,7},{6,4},{7,5}} | collective-permute-start | bytes 5505032 | tf_op jit(solution)/shard_map/ppermute | solution.py:167
  235.3 16.8 %copy-start.19 = (f32[128,3584]{1,0:T(8,128)S(1)}, f32[128,3584]{1,0:T(8,128)}, u32[]{:S(2)}) copy-start(f32[128,3584]{1,0:T(8,128)} %get-tuple-element.30) | copy-start | bytes 5505028
  308.1 176.5 %collective-permute-start.16 = (f32[128,7168]{1,0:T(8,128)}, f32[128,7168]{1,0:T(8,128)}, u32[]{:S(2)}, u32[]{:S(2)}) collective-permute-start(f32[128,7168]{1,0:T(8,128)} %get-tuple-element.38), channel_id=1, source_target_pairs={{0,1},{1,0},{2,3},{3,2},{4,5},{5,4},{6,7},{7,6}} | collective-permute-start | bytes 11010056 | tf_op jit(solution)/shard_map/ppermute | solution.py:164
  331.6 35.9 %copy-start.26 = (s32[2]{0:T(128)S(1)}, s32[2]{0:T(128)}, u32[]{:S(2)}) copy-start(s32[2]{0:T(128)} %param.16) | copy-start | bytes 28
  331.7 42.2 %copy-start.5 = (bf16[2,1024,512]{2,1,0:T(8,128)(2,1)S(1)}, bf16[2,1024,512]{2,1,0:T(8,128)(2,1)}, u32[]{:S(2)}) copy-start(bf16[2,1024,512]{2,1,0:T(8,128)(2,1)} %param.19) | copy-start | bytes 6291460
  361.0 19.2 %copy-start.3 = (bf16[2,512,576]{2,1,0:T(8,128)(2,1)S(1)}, bf16[2,512,576]{2,1,0:T(8,128)(2,1)}, u32[]{:S(2)}) copy-start(bf16[2,512,576]{2,1,0:T(8,128)(2,1)} %copy-done.2) | copy-start | bytes 3538948
  361.0 123.7 %collective-permute-start.13 = (f32[128,7168]{1,0:T(8,128)}, f32[128,7168]{1,0:T(8,128)}, u32[]{:S(2)}, u32[]{:S(2)}) collective-permute-start(f32[128,7168]{1,0:T(8,128)} %get-tuple-element.36), channel_id=1, source_target_pairs={{0,1},{1,0},{2,3},{3,2},{4,5},{5,4},{6,7},{7,6}} | collective-permute-start | bytes 11010056 | tf_op jit(solution)/shard_map/ppermute | solution.py:164
  361.4 45.3 %collective-permute-start.15 = (f32[128,3584]{1,0:T(8,128)}, f32[128,3584]{1,0:T(8,128)}, u32[]{:S(2)}, u32[]{:S(2)}) collective-permute-start(f32[128,3584]{1,0:T(8,128)} %add.124), channel_id=1, source_target_pairs={{0,2},{1,3},{2,0},{3,1},{4,6},{5,7},{6,4},{7,5}} | collective-permute-start | bytes 5505032 | tf_op jit(solution)/shard_map/ppermute | solution.py:167
  365.5 80.5 %collective-permute-start.18 = (f32[128,3584]{1,0:T(8,128)}, f32[128,3584]{1,0:T(8,128)}, u32[]{:S(2)}, u32[]{:S(2)}) collective-permute-start(f32[128,3584]{1,0:T(8,128)} %add.126), channel_id=1, source_target_pairs={{0,2},{1,3},{2,0},{3,1},{4,6},{5,7},{6,4},{7,5}} | collective-permute-start | bytes 5505032 | tf_op jit(solution)/shard_map/ppermute | solution.py:167
  365.5 119.1 %collective-permute-start.17 = (f32[128,3584]{1,0:T(8,128)}, f32[128,3584]{1,0:T(8,128)}, u32[]{:S(2)}, u32[]{:S(2)}) collective-permute-start(f32[128,3584]{1,0:T(8,128)} %add.125), channel_id=1, source_target_pairs={{0,2},{1,3},{2,0},{3,1},{4,6},{5,7},{6,4},{7,5}} | collective-permute-start | bytes 5505032 | tf_op jit(solution)/shard_map/ppermute | solution.py:167
  375.3 11.6 %copy-start.6 = (bf16[1,1024,512]{2,1,0:T(8,128)(2,1)S(1)}, bf16[1,1024,512]{2,1,0:T(8,128)(2,1)}, u32[]{:S(2)}) copy-start(bf16[1,1024,512]{2,1,0:T(8,128)(2,1)} %get-tuple-element.42) | copy-start | bytes 3145732
  380.2 10.5 %copy-start.22 = (bf16[1,1024,64]{1,2,0:T(8,128)(2,1)S(1)}, bf16[1,1024,64]{1,2,0:T(8,128)(2,1)}, u32[]{:S(2)}) copy-start(bf16[1,1024,64]{1,2,0:T(8,128)(2,1)} %dynamic_update_slice.18) | copy-start | bytes 393220
  390.7 94.0 %copy-start.1 = (bf16[2,128,7168]{2,1,0:T(8,128)(2,1)S(1)}, bf16[2,128,7168]{2,1,0:T(8,128)(2,1)}, u32[]{:S(2)}) copy-start(bf16[2,128,7168]{2,1,0:T(8,128)(2,1)} %param.15) | copy-start | bytes 11010052
  (9 other events, 31.5 us)
where the time goes:
time: 504 us; the launch traced here: 495 us
  Pallas kernels  218 us (43%)
  matrix products  104 us (21%)
  waiting for transfers between devices  90.7 us (18%)
  other arithmetic  40 us (8%)
  local copies, waits for them, and re-layouts  22.5 us (4%)
  starting transfers between devices  14.3 us (3%)
  between operations  5.4 us (1%)
    pallas_call x6, Pallas kernels, out_proj(): pl.pallas_call(out_proj_kernel, out_shape=(out, out), grid=(tiles,), in_s...  123 us
    pallas_call x4, Pallas kernels, attention(): pl.pallas_call(functools.partial(attention_kernel, scale=scale), out_shap...  95.4 us
    ppermute x7, waiting for transfers between devices, other_chip(): return lax.ppermute(value, 'tp', to_chip)  90.7 us
    unnamed x3, matrix products  36.8 us
    dot_general x4, matrix products, project(): jnp.einsum('chv,sc->hvs', w_uv, lat, preferred_element_type=F32)  28.9 us
    dot_general x4, matrix products, project(): jnp.einsum('sc,chd->hsd', lat, w_uk, preferred_element_type=F32)  20.9 us
    dot_general x1, matrix products, step(): jnp.dot(normed, w_dq, preferred_element_type=F32)  11.6 us
    ppermute x7, starting transfers between devices, other_chip(): return lax.ppermute(value, 'tp', to_chip)  11.2 us
  transfers between devices with their start and end apart: 19, of which 3 were waited for; matrix products, arithmetic and copies ran while one was open for 29% of the time, Pallas kernels for 44%

commit v1 on v0

v1 whole, which is shorter than its diff:
```python
import functools

import jax
import jax.numpy as jnp
from jax import lax
from jax.experimental import pallas as pl
from jax.experimental.pallas import tpu as pltpu
from jax.sharding import PartitionSpec as P


F32 = jnp.float32
BF16 = jnp.bfloat16
NEG = -1e30
LOG2E = 1.4426950408889634
COL_TILE = 512
COL_CHUNKS = 2
HEADS_PER_STEP = 2
SLOTS = 4
W_SLOTS = 4


def rms_norm(values, gain_vec):
    inv_rms = lax.rsqrt(jnp.mean(values * values, axis=-1, keepdims=True) + 1e-6)
    return values * inv_rms * gain_vec


def apply_rope(values, cos_tab, sin_tab):
    half_dim = values.shape[-1] // 2
    lower_half = values[..., :half_dim]
    upper_half = values[..., half_dim:]
    return jnp.concatenate([lower_half * cos_tab - upper_half * sin_tab, upper_half * cos_tab + lower_half * sin_tab], axis=-1)


def attention_kernel(scal_ref, q_lat_ref, r_ref, cos_ref, sin_ref, w_hbm, k_old_hbm, k_new_hbm, v_old_hbm, v_new_hbm, o_ref,
                     w_buf, k_buf, v_buf, q_lat_t, scores_a, scores_b, top_a, top_b, sems, *, scale):
    step = pl.program_id(0)
    n_steps = pl.num_programs(0)
    m_rows = q_lat_ref.shape[0]
    nope = k_buf.shape[3]
    prefix = k_old_hbm.shape[1]
    rope_half = cos_ref.shape[0]
    blk = m_rows
    half = m_rows // 2
    factor = scale * LOG2E

    def copies(g, slot):
        heads = pl.ds(g * HEADS_PER_STEP, HEADS_PER_STEP)
        pairs = (
            (w_hbm.at[heads], w_buf.at[slot]),
            (k_old_hbm.at[heads], k_buf.at[slot, :, :prefix]),
            (k_new_hbm.at[heads], k_buf.at[slot, :, prefix:]),
            (v_old_hbm.at[heads], v_buf.at[slot, :, :, :prefix]),
            (v_new_hbm.at[heads], v_buf.at[slot, :, :, prefix:]),
        )
        return [pltpu.make_async_copy(src, dst, sems.at[slot, i]) for i, (src, dst) in enumerate(pairs)]

    def fetch(g, slot):
        for copy in copies(g, slot):
            copy.start()

    def arrive(g, slot):
        for copy in copies(g, slot):
            copy.wait()

    def body(new_blocks):
        n_blk = prefix // blk + new_blocks

        def score(slot, h, scores, top):
            q_t = jnp.dot(w_buf[slot, h], q_lat_t[...], preferred_element_type=F32)
            low = q_t[nope:nope + rope_half]
            high = q_t[nope + rope_half:]
            pad_row = lax.broadcasted_iota(jnp.int32, (nope - 2 * rope_half, m_rows), 0)
            q_cat = jnp.concatenate([
                q_t[:nope].astype(BF16),
                (low * cos_ref[...] - high * sin_ref[...]).astype(BF16),
                (high * cos_ref[...] + low * sin_ref[...]).astype(BF16),
                jnp.where(pad_row == 0, 1.0, 0.0).astype(BF16)], axis=0)
            best = None
            for i in range(n_blk):
                rows = slice(i * blk, (i + 1) * blk)
                k_cat = jnp.concatenate([k_buf[slot, h, rows, :], r_ref[rows, :]], axis=1)
                s = jnp.dot(k_cat, q_cat, preferred_element_type=F32)
                if i == n_blk - 1:
                    qlane = lax.broadcasted_iota(jnp.int32, (blk, m_rows), 1)
                    krow = lax.broadcasted_iota(jnp.int32, (blk, m_rows), 0)
                    qpos = jnp.where(qlane < half, scal_ref[0] * half + qlane, scal_ref[1] * half + qlane - half)
                    s = jnp.where(krow <= qpos - scal_ref[2] * m_rows, s, NEG)
                scores[rows, :] = s
                top_i = jnp.max(s, axis=0, keepdims=True)
                best = top_i if best is None else jnp.maximum(best, top_i)
            top[...] = best

        def finish(slot, h, scores, top):
            best = top[...]
            total = None
            out = None
            for i in range(n_blk):
                rows = slice(i * blk, (i + 1) * blk)
                e = jnp.exp2((scores[rows, :] - best) * factor)
                part = jnp.sum(e, axis=0, keepdims=True)
                total = part if total is None else total + part
                o_part = jnp.dot(v_buf[slot, h, :, rows], e.astype(BF16), preferred_element_type=F32)
                out = o_part if out is None else out + o_part
            out = out * (1.0 / total)
            o_ref[:, h * nope:(h + 1) * nope] = out.T.astype(BF16)

        @pl.when(step == 0)
        def _():
            for g in range(SLOTS):
                fetch(g, g)
            q_lat_t[...] = q_lat_ref[...].T
            arrive(0, 0)
            score(0, 0, scores_a, top_a)

        slot = lax.rem(step, SLOTS)
        following = jnp.minimum(step + 1, n_steps - 1)
        next_slot = lax.rem(following, SLOTS)
        score(slot, 1, scores_b, top_b)
        finish(slot, 0, scores_a, top_a)

        @pl.when(step + 1 < n_steps)
        def _():
            arrive(step + 1, next_slot)

        score(next_slot, 0, scores_a, top_a)
        finish(slot, 1, scores_b, top_b)

        @pl.when(step + SLOTS < n_steps)
        def _():
            fetch(step + SLOTS, slot)

    for c in range((k_buf.shape[2] - prefix) // blk):
        @pl.when(scal_ref[2] == c)
        def _(c=c):
            body(c + 1)


def attention(scal, q_lat, w_t, k_old, k_new, v_old, v_new, r_cat, cos_tab, sin_tab, scale):
    n_heads, q_dim, q_rank = w_t.shape
    m_rows = q_lat.shape[0]
    prefix, nope = k_old.shape[1:]
    n_keys = prefix + k_new.shape[1]
    hb = HEADS_PER_STEP
    flops = 2 * n_heads * m_rows * (n_keys * (256 + 128) + q_dim * q_rank)
    whole = lambda arr: pl.BlockSpec(arr.shape, lambda g, s: (0, 0))
    raw = pl.BlockSpec(memory_space=pl.ANY)
    return pl.pallas_call(
        functools.partial(attention_kernel, scale=scale),
        out_shape=jax.ShapeDtypeStruct((m_rows, n_heads * nope), BF16),
        grid_spec=pltpu.PrefetchScalarGridSpec(
            num_scalar_prefetch=1,
            grid=(n_heads // hb,),
            in_specs=[whole(q_lat), whole(r_cat), whole(cos_tab), whole(sin_tab), raw, raw, raw, raw, raw],
            out_specs=pl.BlockSpec((m_rows, hb * nope), lambda g, s: (0, g)),
            scratch_shapes=[
                pltpu.VMEM((SLOTS, hb, q_dim, q_rank), BF16),
                pltpu.VMEM((SLOTS, hb, n_keys, nope), BF16),
                pltpu.VMEM((SLOTS, hb, nope, n_keys), BF16),
                pltpu.VMEM((q_rank, m_rows), BF16),
                pltpu.VMEM((n_keys, m_rows), F32),
                pltpu.VMEM((n_keys, m_rows), F32),
                pltpu.VMEM((1, m_rows), F32),
                pltpu.VMEM((1, m_rows), F32),
                pltpu.SemaphoreType.DMA((SLOTS, 5)),
            ],
        ),
        compiler_params=pltpu.CompilerParams(dimension_semantics=("arbitrary",)),
        cost_estimate=pl.CostEstimate(flops=flops, bytes_accessed=38_000_000, transcendentals=n_heads * m_rows * n_keys),
        name="attention",
    )(scal, q_lat, r_cat, cos_tab, sin_tab, w_t, k_old, k_new, v_old, v_new)


def out_proj_kernel(*refs, n_in, first):
    o_hbm = refs[:n_in]
    w_hbm, near_ref, far_ref, o_buf, w_buf, o_sems, w_sems = refs[n_in:]
    j = pl.program_id(0)
    tiles = pl.num_programs(0)
    slots = w_buf.shape[0]
    half = o_buf.shape[1] // 2

    def weights(tile, slot):
        col = pl.multiple_of((tile + first) * COL_TILE, COL_TILE)
        return pltpu.make_async_copy(w_hbm.at[:, pl.ds(col, COL_TILE)], w_buf.at[slot], w_sems.at[slot])

    @pl.when(j == 0)
    def _():
        weights(0, 0).start()
        loads = [pltpu.make_async_copy(o_hbm[i], o_buf.at[i], o_sems.at[i]) for i in range(n_in)]
        for load in loads:
            load.start()
        for slot in range(1, slots):
            weights(slot, slot).start()
        for load in loads:
            load.wait()

    slot = lax.rem(j, slots)
    weights(j, slot).wait()
    for i in range(n_in):
        prod = jnp.dot(o_buf[i], w_buf[slot], preferred_element_type=F32)
        near_ref[i * half:(i + 1) * half, :] = prod[:half]
        far_ref[i * half:(i + 1) * half, :] = prod[half:]

    @pl.when(j + slots < tiles)
    def _():
        weights(j + slots, slot).start()


def out_proj(o_list, w_out, first, count):
    m_rows, depth = o_list[0].shape
    n_in = len(o_list)
    half = m_rows // 2
    tiles = count // COL_TILE
    out = jax.ShapeDtypeStruct((n_in * half, count), F32)
    raw = pl.BlockSpec(memory_space=pl.ANY)
    out_spec = pl.BlockSpec((n_in * half, COL_TILE), lambda j: (0, j))
    return pl.pallas_call(
        functools.partial(out_proj_kernel, n_in=n_in, first=first // COL_TILE),
        out_shape=(out, out),
        grid=(tiles,),
        in_specs=[raw] * (n_in + 1),
        out_specs=(out_spec, out_spec),
        scratch_shapes=[
            pltpu.VMEM((n_in, m_rows, depth), BF16),
            pltpu.VMEM((W_SLOTS, depth, COL_TILE), BF16),
            pltpu.SemaphoreType.DMA((n_in,)),
            pltpu.SemaphoreType.DMA((W_SLOTS,)),
        ],
        compiler_params=pltpu.CompilerParams(dimension_semantics=("arbitrary",)),
        cost_estimate=pl.CostEstimate(flops=2 * n_in * m_rows * depth * count, bytes_accessed=depth * count * 2 + n_in * m_rows * count * 4, transcendentals=0),
        name="out_proj",
    )(*o_list, w_out)


def solution(mesh):
    tp = mesh.shape["tp"]
    to_partner = [(i, i ^ 1) for i in range(tp)]
    to_chip = [(i, i ^ 2) for i in range(tp)]

    def partner(value):
        return lax.ppermute(value, "tp", to_partner)

    def other_chip(value):
        return lax.ppermute(value, "tp", to_chip)

    def step(hidden, lengths, rope_cos, rope_sin, cache_lat, cache_pe, norm_in, w_dq, norm_q, w_dkv, norm_kv, w_uq, w_uk, w_uv, w_out):
        me = lax.axis_index("tp")
        n_seq, n_tok, model_dim = hidden.shape
        kv_rank, _, nope = w_uk.shape
        rope_dim = cache_pe.shape[2]
        n_new = rope_cos.shape[1]
        prefix = cache_lat.shape[1] - n_new
        q_rank = w_dq.shape[1]
        scale = (nope + rope_dim) ** -0.5

        normed = rms_norm(hidden.astype(F32), norm_in).astype(BF16).reshape(n_seq * n_tok, model_dim)
        kv_proj = jnp.dot(normed, w_dkv, preferred_element_type=F32).reshape(n_seq, n_tok, kv_rank + rope_dim)
        my_cos = lax.dynamic_slice_in_dim(rope_cos, me * n_tok, n_tok, axis=1)
        my_sin = lax.dynamic_slice_in_dim(rope_sin, me * n_tok, n_tok, axis=1)
        my_lat = rms_norm(kv_proj[..., :kv_rank], norm_kv).astype(BF16)
        my_pe = apply_rope(kv_proj[..., kv_rank:], my_cos, my_sin).astype(BF16)
        my_kv = jnp.concatenate([my_lat, my_pe], axis=-1)
        my_q = rms_norm(jnp.dot(normed, w_dq, preferred_element_type=F32), norm_q).astype(BF16).reshape(n_seq, n_tok, q_rank)

        def gather(value):
            far = other_chip(value)
            near = partner(value)
            return [value, near, far, partner(far)]

        kv_rel = jnp.stack(gather(my_kv))
        kv_true = jnp.concatenate([lax.dynamic_index_in_dim(kv_rel, me ^ j, keepdims=False) for j in range(tp)], axis=1)
        lat_new = kv_true[..., :kv_rank]
        pe_new = kv_true[..., kv_rank:]
        q_rel = [gather(my_q[b]) for b in range(n_seq)]

        def project(lat):
            keys = jnp.einsum("sc,chd->hsd", lat, w_uk, preferred_element_type=F32).astype(BF16)
            values = jnp.einsum("chv,sc->hvs", w_uv, lat, preferred_element_type=F32).astype(BF16)
            return keys, values

        row = jnp.arange(prefix)
        alive = row[None, :] < lengths[:, None]
        old_lat = jnp.where(alive[..., None], cache_lat[:, :prefix], 0)
        old_pe = jnp.where(alive[..., None], cache_pe[:, :prefix], 0)
        kv_old = [project(old_lat[b]) for b in range(n_seq)]
        kv_new = [project(lat_new[b]) for b in range(n_seq)]
        bias = jnp.where(alive, 0.0, NEG).astype(BF16)[..., None]
        pad_old = jnp.zeros((n_seq, prefix, nope - rope_dim - 1), BF16)
        pad_new = jnp.zeros((n_seq, n_new, nope - rope_dim), BF16)
        r_cat = jnp.concatenate([
            jnp.concatenate([old_pe, bias, pad_old], axis=-1),
            jnp.concatenate([pe_new, pad_new], axis=-1)], axis=1)

        w_t = w_uq.transpose(1, 2, 0)

        def attend(rel, b, q_lat):
            blocks = (me ^ rel, me ^ (rel + 1))
            scal = jnp.stack([blocks[0], blocks[1], blocks[0] // 2]).astype(jnp.int32)
            cut = lambda tab: jnp.concatenate([lax.dynamic_slice_in_dim(tab[b], k * n_tok, n_tok, axis=0) for k in blocks], axis=0).T
            return attention(scal, q_lat, w_t, kv_old[b][0], kv_new[b][0], kv_old[b][1], kv_new[b][1], r_cat[b], cut(rope_cos), cut(rope_sin), scale)

        def after(value, *deps):
            return lax.optimization_barrier((value,) + deps)[0]

        width = model_dim // COL_CHUNKS
        arrived = [[None] * COL_CHUNKS for _ in range(n_seq)]
        pending = []

        def send_one():
            b, j, near_part, came = pending.pop(0)
            summed = near_part + came
            arrived[b][j] = other_chip(summed)
            return summed

        near_part = None
        for b in range(n_seq):
            q_lat = jnp.concatenate(q_rel[b][2:], axis=0)
            if near_part is not None:
                q_lat = after(q_lat, near_part, send_one())
            o = attend(2, b, q_lat)
            for j in range(COL_CHUNKS):
                if len(pending) > 1 - (j == 0):
                    o = after(o, send_one())
                near_part, far_part = out_proj([o], w_out, j * width, width)
                pending.append((b, j, near_part, partner(far_part)))
        dep = (near_part, send_one())
        o_own = []
        for b in range(n_seq):
            q_lat = after(jnp.concatenate(q_rel[b][:2], axis=0), *dep)
            o_own.append(attend(0, b, q_lat))
            dep = (o_own[-1],) + ((send_one(),) if pending else ())
        cols = []
        flat = hidden.reshape(n_seq * n_tok, model_dim)
        for j in range(COL_CHUNKS):
            own_part, partner_part = out_proj([after(o_own[0], *dep), o_own[1]], w_out, j * width, width)
            dep = (own_part,)
            base = own_part + partner(partner_part) + flat[:, j * width:(j + 1) * width].astype(F32)
            cols.append(base + jnp.concatenate([arrived[b][j] for b in range(n_seq)], axis=0))
        out = jnp.concatenate(cols, axis=1).astype(BF16).reshape(hidden.shape)
        lat_all = jnp.stack([lax.dynamic_update_slice(cache_lat[b], lat_new[b], (lengths[b], 0)) for b in range(n_seq)])
        pe_all = jnp.stack([lax.dynamic_update_slice(cache_pe[b], pe_new[b], (lengths[b], 0)) for b in range(n_seq)])
        return out, lat_all, pe_all

    spec_tok = P("dp", "tp", None)
    spec_len = P("dp")
    spec_seq = P("dp", None, None)
    spec_vec = P(None)
    spec_mat = P(None, None)
    spec_head = P(None, "tp", None)
    spec_rows = P("tp", None)
    in_specs = (spec_tok, spec_len, spec_seq, spec_seq, spec_seq, spec_seq, spec_vec, spec_mat, spec_vec, spec_mat, spec_vec, spec_head, spec_head, spec_head, spec_rows)
    return jax.shard_map(step, mesh=mesh, in_specs=in_specs, out_specs=(spec_tok, spec_seq, spec_seq), check_vma=False)
```

time: 504 us -> 519 us (1.030)
  Pallas kernels: 218 us -> 258 us
  matrix products: 104 us -> 68.6 us
  other arithmetic: 40 us -> 50.2 us
    pallas_call x4, Pallas kernels: 95.4 us -> 151 us  [attention(): pl.pallas_call(functools.partial(attention_kernel, scale=scale), out_shap...]
    unnamed x3 -> x0, matrix products: 36.8 us -> none
    pallas_call x6, Pallas kernels: 123 us -> 107 us  [out_proj(): pl.pallas_call(functools.partial(out_proj_kernel, n_in=n_in, first=first...]
    another operation x3 -> x2, other arithmetic: 11.4 us -> 8.35 us  [the longest x2 10.6 us: step(): out = jnp.stack(result)]
  transfers between devices with their start and end apart: 19 -> 19, of which waited for: 3 -> 3; matrix products, arithmetic and copies ran while one was open for 29% -> 23% of each run, Pallas kernels for 44% -> 47%
where the time goes in v1:
time: 519 us; the launch traced here: 513 us
  Pallas kernels  258 us (50%)
  waiting for transfers between devices  90.9 us (18%)
  matrix products  68.6 us (13%)
  other arithmetic  50.2 us (10%)
  local copies, waits for them, and re-layouts  23.6 us (5%)
  starting transfers between devices  16.4 us (3%)
  between operations  5.66 us (1%)
    pallas_call x4, Pallas kernels, attention(): pl.pallas_call(functools.partial(attention_kernel, scale=scale), out_shap...  151 us
    pallas_call x6, Pallas kernels, out_proj(): pl.pallas_call(functools.partial(out_proj_kernel, n_in=n_in, first=first...  107 us
    ppermute x7, waiting for transfers between devices, other_chip(): return lax.ppermute(value, 'tp', to_chip)  90.9 us
    dot_general x4, matrix products, project(): jnp.einsum('chv,sc->hvs', w_uv, lat, preferred_element_type=F32)  30 us
    dot_general x4, matrix products, project(): jnp.einsum('sc,chd->hsd', lat, w_uk, preferred_element_type=F32)  20.8 us
    ppermute x7, starting transfers between devices, other_chip(): return lax.ppermute(value, 'tp', to_chip)  13.7 us
    dot_general x1, matrix products, step(): jnp.dot(normed, w_dq, preferred_element_type=F32)  11.6 us
  transfers between devices with their start and end apart: 19, of which 3 were waited for; matrix products, arithmetic and copies ran while one was open for 23% of the time, Pallas kernels for 47%

profile of v1, /device:TPU:0, one launch (start us, length us, event | category | flops | bytes accessed | tf_op | source)
XLA Modules:
  0.0 513.0 jit_solution(7054744454630371987)
XLA Ops:
  0.6 3.0 fusion.2
  3.8 1.8 fusion.4
  5.6 6.2 %fusion = f32[2,128,576]{1,2,0:T(8,128)S(1)} fusion(bf16[2,128,7168]{2,1,0:T(8,128)(2,1)S(1)} %fusion.4, bf16[7168,576]{0,1:T(8,128)(2,1)} %param.24), kind=kOutput, calls=%fused_computation.2 | convolution fusion | flops 2113929216 | bytes 12517376 | tf_op jit(solution)/shard_map/dot_general | solution.py:256
  12.9 3.3 collective-permute-start.6
  16.2 11.6 %multiply_reduce_fusion = (f32[256]{0:T(256)S(1)}, f32[256,1536]{1,0:T(8,128)S(1)}) fusion(bf16[256,7168]{1,0:T(8,128)(2,1)} %bitcast.121, bf16[7168,1536]{1,0:T(8,128)(2,1)} %param.22), kind=kOutput, calls=%fused_computation.38 | convolution fusion | flops 5637931008 | bytes 27264000 | tf_op jit(solution)/shard_map/dot_general | solution.py:262
  28.9 2.0 collective-permute-start.1
  31.3 8.1 %convert_bitcast_fusion.5.v_old_hbm = bf16[32,128,512]{2,1,0:T(8,128)(2,1)} fusion(bf16[512,32,128]{2,1,0:T(8,128)(2,1)} %param.28, bf16[2,512,512]{2,1,0:T(8,128)(2,1)S(1)} %slice_select_fusion), kind=kOutput, calls=%fused_computation.12 | convolution fusion | flops 2149580800 | bytes 8912896 | tf_op jit(solution)/shard_map/chv,sc->hvs/dot_general | solution.py:277
  39.4 6.0 %convert_bitcast_fusion.1.v_old_hbm = bf16[32,128,512]{2,1,0:T(8,128)(2,1)} fusion(bf16[512,32,128]{2,1,0:T(8,128)(2,1)S(1)} %copy-done.36, bf16[2,512,512]{2,1,0:T(8,128)(2,1)S(1)} %slice_select_fusion), kind=kOutput, calls=%fused_computation.8 | convolution fusion | flops 2149580800 | bytes 8912896 | tf_op jit(solution)/shard_map/chv,sc->hvs/dot_general | solution.py:277
  45.4 4.4 convert_bitcast_fusion.7.k_old_hbm
  49.8 5.0 convert_bitcast_fusion.3.k_old_hbm
  64.8 8.1 %convert_bitcast_fusion.4.v_new_hbm = bf16[32,128,512]{2,1,0:T(8,128)(2,1)} fusion(bf16[512,32,128]{2,1,0:T(8,128)(2,1)} %param.28, bf16[2,512,576]{2,1,0:T(8,128)(2,1)S(1)} %pad_maximum_fusion.2), kind=kOutput, calls=%fused_computation.11 | convolution fusion | flops 2149580800 | bytes 8912896 | tf_op jit(solution)/shard_map/chv,sc->hvs/dot_general | solution.py:277
  74.0 4.6 convert_bitcast_fusion.6.k_new_hbm
  78.6 2.0 pad_maximum_fusion.6.q_lat_ref
  80.6 38.8 %attention.4.refs_0_ = bf16[256,4096]{1,0:T(8,128)(2,1)} custom-call(s32[3]{0:T(128)} %pad_add_fusion.1.scal_ref, bf16[256,1536]{1,0:T(8,128)(2,1)} %pad_maximum_fusion.6.q_lat_ref, bf16[1024,128]{1,0:T(8,128)(2,1)} %get-tuple-element.56.r_ref, f32[32,256]{1,0:T(8,128)} %maximum_bitcast_fusion.cos_ref, f32[32,256]{1,0:T(8,128)} %maximum_bitcast_fusion.1.sin_ref, ...), custom_call_target="tpu_custom_call" | custom-call | flops 11274289152 | bytes 38000000 | tf_op jit(solution)/shard_map/attention/pallas_call | solution.py:147
  119.5 14.9 %out_proj.7 = (f32[128,3584]{1,0:T(8,128)}, f32[128,3584]{1,0:T(8,128)}) custom-call(bf16[256,4096]{1,0:T(8,128)(2,1)} %attention.4.refs_0_, bf16[4096,7168]{1,0:T(8,128)(2,1)} %refs_2_.3), custom_call_target="tpu_custom_call" | custom-call | flops 7516192768 | bytes 33030144 | tf_op jit(solution)/shard_map/out_proj/pallas_call | solution.py:216
  134.9 7.8 %convert_bitcast_fusion.v_new_hbm = bf16[32,128,512]{2,1,0:T(8,128)(2,1)} fusion(bf16[512,32,128]{2,1,0:T(8,128)(2,1)} %param.28, bf16[2,512,576]{2,1,0:T(8,128)(2,1)S(1)} %pad_maximum_fusion.2), kind=kOutput, calls=%fused_computation.7 | convolution fusion | flops 2149580800 | bytes 8912896 | tf_op jit(solution)/shard_map/chv,sc->hvs/dot_general | solution.py:277
  142.7 14.9 %out_proj.6 = (f32[128,3584]{1,0:T(8,128)}, f32[128,3584]{1,0:T(8,128)}) custom-call(bf16[256,4096]{1,0:T(8,128)(2,1)} %attention.4.refs_0_, bf16[4096,7168]{1,0:T(8,128)(2,1)} %refs_2_.3), custom_call_target="tpu_custom_call" | custom-call | flops 7516192768 | bytes 33030144 | tf_op jit(solution)/shard_map/out_proj/pallas_call | solution.py:216
  157.7 6.9 %convert_bitcast_fusion.2.k_new_hbm = bf16[32,512,128]{2,1,0:T(8,128)(2,1)} fusion(bf16[512,32,128]{2,1,0:T(8,128)(2,1)} %param.27, bf16[2,512,576]{2,1,0:T(8,128)(2,1)S(1)} %pad_maximum_fusion.2), kind=kOutput, calls=%fused_computation.9 | convolution fusion | flops 2149580800 | bytes 8912896 | tf_op jit(solution)/shard_map/sc,chd->hsd/dot_general | solution.py:276
  164.6 2.0 pad_maximum_fusion.5.q_lat_ref
  166.6 1.5 add.123
  168.1 39.0 %attention.5.refs_0_ = bf16[256,4096]{1,0:T(8,128)(2,1)} custom-call(s32[3]{0:T(128)} %pad_add_fusion.1.scal_ref, bf16[256,1536]{1,0:T(8,128)(2,1)} %pad_maximum_fusion.5.q_lat_ref, bf16[1024,128]{1,0:T(8,128)(2,1)} %get-tuple-element.55.r_ref, f32[32,256]{1,0:T(8,128)} %maximum_bitcast_fusion.2.cos_ref, f32[32,256]{1,0:T(8,128)} %maximum_bitcast_fusion.3.sin_ref, ...), custom_call_target="tpu_custom_call" | custom-call | flops 11274289152 | bytes 38000000 | tf_op jit(solution)/shard_map/attention/pallas_call | solution.py:147
  207.1 3.0 add.124
  210.1 15.0 %out_proj.9 = (f32[128,3584]{1,0:T(8,128)}, f32[128,3584]{1,0:T(8,128)}) custom-call(bf16[256,4096]{1,0:T(8,128)(2,1)} %attention.5.refs_0_, bf16[4096,7168]{1,0:T(8,128)(2,1)} %refs_2_.3), custom_call_target="tpu_custom_call" | custom-call | flops 7516192768 | bytes 33030144 | tf_op jit(solution)/shard_map/out_proj/pallas_call | solution.py:216
  227.2 15.0 %out_proj.8 = (f32[128,3584]{1,0:T(8,128)}, f32[128,3584]{1,0:T(8,128)}) custom-call(bf16[256,4096]{1,0:T(8,128)(2,1)} %attention.5.refs_0_, bf16[4096,7168]{1,0:T(8,128)(2,1)} %refs_2_.3), custom_call_target="tpu_custom_call" | custom-call | flops 7516192768 | bytes 33030144 | tf_op jit(solution)/shard_map/out_proj/pallas_call | solution.py:216
  245.7 2.1 pad_maximum_fusion.4.q_lat_ref
  247.8 2.0 pad_maximum_fusion.7.q_lat_ref
  249.7 2.9 add.125
  252.7 36.6 %attention.6.refs_0_ = bf16[256,4096]{1,0:T(8,128)(2,1)} custom-call(s32[3]{0:T(128)} %pad_add_fusion.scal_ref, bf16[256,1536]{1,0:T(8,128)(2,1)} %pad_maximum_fusion.4.q_lat_ref, bf16[1024,128]{1,0:T(8,128)(2,1)} %get-tuple-element.56.r_ref, f32[32,256]{1,0:T(8,128)} %maximum_bitcast_fusion.4.cos_ref, f32[32,256]{1,0:T(8,128)} %maximum_bitcast_fusion.5.sin_ref, ...), custom_call_target="tpu_custom_call" | custom-call | flops 11274289152 | bytes 38000000 | tf_op jit(solution)/shard_map/attention/pallas_call | solution.py:147
  289.3 2.9 add.127
  292.2 36.7 %attention.7.refs_1_ = bf16[256,4096]{1,0:T(8,128)(2,1)} custom-call(s32[3]{0:T(128)} %pad_add_fusion.scal_ref, bf16[256,1536]{1,0:T(8,128)(2,1)} %pad_maximum_fusion.7.q_lat_ref, bf16[1024,128]{1,0:T(8,128)(2,1)} %get-tuple-element.55.r_ref, f32[32,256]{1,0:T(8,128)} %maximum_bitcast_fusion.6.cos_ref, f32[32,256]{1,0:T(8,128)} %maximum_bitcast_fusion.7.sin_ref, ...), custom_call_target="tpu_custom_call" | custom-call | flops 11274289152 | bytes 38000000 | tf_op jit(solution)/shard_map/attention/pallas_call | solution.py:147
  329.0 23.3 %out_proj.10 = (f32[256,3584]{1,0:T(8,128)}, f32[256,3584]{1,0:T(8,128)}) custom-call(bf16[256,4096]{1,0:T(8,128)(2,1)} %attention.6.refs_0_, bf16[256,4096]{1,0:T(8,128)(2,1)} %attention.7.refs_1_, bf16[4096,7168]{1,0:T(8,128)(2,1)} %refs_2_.3), custom_call_target="tpu_custom_call" | custom-call | flops 15032385536 | bytes 36700160 | tf_op jit(solution)/shard_map/out_proj/pallas_call | solution.py:216
  352.3 23.5 %out_proj.11 = (f32[256,3584]{1,0:T(8,128)}, f32[256,3584]{1,0:T(8,128)}) custom-call(bf16[256,4096]{1,0:T(8,128)(2,1)} %attention.6.refs_0_, bf16[256,4096]{1,0:T(8,128)(2,1)} %attention.7.refs_1_, bf16[4096,7168]{1,0:T(8,128)(2,1)} %refs_2_.3), custom_call_target="tpu_custom_call" | custom-call | flops 15032385536 | bytes 36700160 | tf_op jit(solution)/shard_map/out_proj/pallas_call | solution.py:216
  376.3 6.3 %collective-permute-start.14 = (f32[128,3584]{1,0:T(8,128)}, f32[128,3584]{1,0:T(8,128)}, u32[]{:S(2)}, u32[]{:S(2)}) collective-permute-start(f32[128,3584]{1,0:T(8,128)} %add.123), channel_id=1, source_target_pairs={{0,2},{1,3},{2,0},{3,1},{4,6},{5,7},{6,4},{7,5}} | collective-permute-start | bytes 5505032 | tf_op jit(solution)/shard_map/ppermute | solution.py:243
  382.7 2.0 collective-permute-start.15
  389.2 1.8 fusion.53
  391.0 1.5 fusion.50
  393.2 1.6 copy.35
  395.6 1.8 dynamic_update_slice.18
  398.4 4.0 dynamic_update_slice.16
  402.5 1.6 dynamic_update_slice.19
  404.0 3.8 dynamic_update_slice.17
  407.8 1.8 pad_maximum_fusion.9
  409.6 1.5 pad_maximum_fusion.1
  411.1 12.7 %collective-permute-done.14 = f32[128,3584]{1,0:T(8,128)} collective-permute-done((f32[128,3584]{1,0:T(8,128)}, f32[128,3584]{1,0:T(8,128)}, u32[]{:S(2)}, u32[]{:S(2)}) %collective-permute-start.14) | collective-permute-done | bytes 1835040 | tf_op jit(solution)/shard_map/ppermute | solution.py:243
  423.9 39.3 %collective-permute-done.18 = f32[128,3584]{1,0:T(8,128)} collective-permute-done((f32[128,3584]{1,0:T(8,128)}, f32[128,3584]{1,0:T(8,128)}, u32[]{:S(2)}, u32[]{:S(2)}) %collective-permute-start.18) | collective-permute-done | bytes 1835040 | tf_op jit(solution)/shard_map/ppermute | solution.py:243
  463.2 38.8 %collective-permute-done.15 = f32[128,3584]{1,0:T(8,128)} collective-permute-done((f32[128,3584]{1,0:T(8,128)}, f32[128,3584]{1,0:T(8,128)}, u32[]{:S(2)}, u32[]{:S(2)}) %collective-permute-start.15) | collective-permute-done | bytes 1835040 | tf_op jit(solution)/shard_map/ppermute | solution.py:243
  502.0 8.3 %fusion.5 = (bf16[256,3584]{1,0:T(8,128)(2,1)S(1)}, bf16[256,3584]{1,0:T(8,128)(2,1)S(1)}) fusion(f32[128,3584]{1,0:T(8,128)} %collective-permute-done.15, f32[128,3584]{1,0:T(8,128)} %collective-permute-done.14, f32[256,3584]{1,0:T(8,128)} %get-tuple-element.34, f32[256,3584]{1,0:T(8,128)} %collective-permute-done.13, bf16[256,7168]{1,0:T(8,128)(2,1)S(1)} %bitcast.118, ...), kind=kLoop, calls=%fused_computation.16 | loop fusion | flops 11010048 | bytes 29360128 | tf_op jit(solution)/shard_map/convert.3
  510.3 2.3 pad_maximum_fusion
  (155 shorter events, 23.4 us)
Async XLA Ops:
  5.6 6.5 %copy-start.23 = (f32[2,512,32]{1,2,0:T(8,128)S(1)}, f32[2,512,32]{1,2,0:T(8,128)}, u32[]{:S(2)}) copy-start(f32[2,512,32]{1,2,0:T(8,128)} %param.18) | copy-start | bytes 393220
  5.6 6.5 %copy-start.24 = (f32[2,512,32]{1,2,0:T(8,128)S(1)}, f32[2,512,32]{1,2,0:T(8,128)}, u32[]{:S(2)}) copy-start(f32[2,512,32]{1,2,0:T(8,128)} %param.17) | copy-start | bytes 393220
  12.9 47.5 %collective-permute-start.6 = (bf16[2,128,576]{1,2,0:T(8,128)(2,1)}, bf16[2,128,576]{1,2,0:T(8,128)(2,1)S(1)}, u32[]{:S(2)}, u32[]{:S(2)}) collective-permute-start(bf16[2,128,576]{1,2,0:T(8,128)(2,1)} %get-tuple-element.58), channel_id=1, source_target_pairs={{0,2},{1,3},{2,0},{3,1},{4,6},{5,7},{6,4},{7,5}} | collective-permute-start | bytes 884744 | tf_op jit(solution)/shard_map/ppermute | solution.py:243
  16.2 46.3 %collective-permute-start.5 = (bf16[2,128,576]{1,2,0:T(8,128)(2,1)}, bf16[2,128,576]{1,2,0:T(8,128)(2,1)}, u32[]{:S(2)}, u32[]{:S(2)}) collective-permute-start(bf16[2,128,576]{1,2,0:T(8,128)(2,1)} %get-tuple-element.58), channel_id=1, source_target_pairs={{0,1},{1,0},{2,3},{3,2},{4,5},{5,4},{6,7},{7,6}} | collective-permute-start | bytes 884744 | tf_op jit(solution)/shard_map/ppermute | solution.py:240
  16.2 11.7 %copy-start.31 = (f32[1536]{0:T(1024)S(1)}, f32[1536]{0:T(1024)}, u32[]{:S(2)}) copy-start(f32[1536]{0:T(1024)} %param.23) | copy-start | bytes 18436
  28.9 33.0 %collective-permute-start.3 = (bf16[128,1536]{1,0:T(8,128)(2,1)}, bf16[128,1536]{1,0:T(8,128)(2,1)}, u32[]{:S(2)}, u32[]{:S(2)}) collective-permute-start(bf16[128,1536]{1,0:T(8,128)(2,1)} %get-tuple-element.53), channel_id=1, source_target_pairs={{0,2},{1,3},{2,0},{3,1},{4,6},{5,7},{6,4},{7,5}} | collective-permute-start | bytes 1179656 | tf_op jit(solution)/shard_map/ppermute | solution.py:243
  28.9 33.5 %collective-permute-start.1 = (bf16[128,1536]{1,0:T(8,128)(2,1)S(1)}, bf16[128,1536]{1,0:T(8,128)(2,1)}, u32[]{:S(2)}, u32[]{:S(2)}) collective-permute-start(bf16[128,1536]{1,0:T(8,128)(2,1)S(1)} %get-tuple-element.54), channel_id=1, source_target_pairs={{0,2},{1,3},{2,0},{3,1},{4,6},{5,7},{6,4},{7,5}} | collective-permute-start | bytes 1179656 | tf_op jit(solution)/shard_map/ppermute | solution.py:243
  31.1 8.3 %copy-start.29 = (pred[2,512]{1,0:T(4,128)(4,1)}, pred[2,512]{1,0:T(4,128)(4,1)S(1)}, u32[]{:S(2)}) copy-start(pred[2,512]{1,0:T(4,128)(4,1)S(1)} %iota_compare_fusion.2) | copy-start | bytes 3076
  31.3 8.1 %copy-start.36 = (bf16[512,32,128]{2,1,0:T(8,128)(2,1)S(1)}, bf16[512,32,128]{2,1,0:T(8,128)(2,1)}, u32[]{:S(2)}) copy-start(bf16[512,32,128]{2,1,0:T(8,128)(2,1)} %param.28) | copy-start | bytes 12582916
  49.8 8.0 %copy-start.33 = (s32[2]{0:T(128)S(1)}, s32[2]{0:T(128)}, u32[]{:S(2)}) copy-start(s32[2]{0:T(128)} %param.16) | copy-start | bytes 28
  49.8 9.5 %slice-start = ((bf16[2,1024,64]{1,2,0:T(8,128)(2,1)}), bf16[2,512,64]{1,2,0:T(8,128)(2,1)S(1)}, s32[]{:S(2)}) async-start(bf16[2,1024,64]{1,2,0:T(8,128)(2,1)} %param.20), calls=%async_computation | async-start | bytes 262144 | tf_op jit(solution)/shard_map/slice | solution.py:283
  49.8 11.2 %copy-start.30 = (pred[2,512]{1,0:T(4,128)(4,1)S(1)}, pred[2,512]{1,0:T(4,128)(4,1)}, u32[]{:S(2)}) copy-start(pred[2,512]{1,0:T(4,128)(4,1)} %copy-done.29) | copy-start | bytes 3076
  60.4 2.1 collective-permute-start.7
  62.0 16.6 %collective-permute-start.4 = (bf16[128,1536]{1,0:T(8,128)(2,1)}, bf16[128,1536]{1,0:T(8,128)(2,1)}, u32[]{:S(2)}, u32[]{:S(2)}) collective-permute-start(bf16[128,1536]{1,0:T(8,128)(2,1)} %collective-permute-done.3), channel_id=1, source_target_pairs={{0,1},{1,0},{2,3},{3,2},{4,5},{5,4},{6,7},{7,6}} | collective-permute-start | bytes 1179656 | tf_op jit(solution)/shard_map/ppermute | solution.py:240
  62.5 102.1 %collective-permute-start.2 = (bf16[128,1536]{1,0:T(8,128)(2,1)}, bf16[128,1536]{1,0:T(8,128)(2,1)}, u32[]{:S(2)}, u32[]{:S(2)}) collective-permute-start(bf16[128,1536]{1,0:T(8,128)(2,1)} %collective-permute-done.1), channel_id=1, source_target_pairs={{0,1},{1,0},{2,3},{3,2},{4,5},{5,4},{6,7},{7,6}} | collective-permute-start | bytes 1179656 | tf_op jit(solution)/shard_map/ppermute | solution.py:240
  63.9 8.9 %copy-start.7 = (bf16[1,2,128,576]{3,2,1,0:T(8,128)(2,1)}, bf16[1,2,128,576]{3,2,1,0:T(8,128)(2,1)S(1)}, u32[]{:S(2)}) copy-start(bf16[1,2,128,576]{3,2,1,0:T(8,128)(2,1)S(1)} %copy.19) | copy-start | bytes 884740
  64.1 8.7 %copy-start.9 = (bf16[1,2,128,576]{3,2,1,0:T(8,128)(2,1)}, bf16[1,2,128,576]{3,2,1,0:T(8,128)(2,1)S(1)}, u32[]{:S(2)}) copy-start(bf16[1,2,128,576]{3,2,1,0:T(8,128)(2,1)S(1)} %copy.20) | copy-start | bytes 884740
  64.4 8.5 %copy-start.11 = (bf16[1,2,128,576]{3,2,1,0:T(8,128)(2,1)}, bf16[1,2,128,576]{3,2,1,0:T(8,128)(2,1)S(1)}, u32[]{:S(2)}) copy-start(bf16[1,2,128,576]{3,2,1,0:T(8,128)(2,1)S(1)} %copy.21) | copy-start | bytes 884740
  64.6 8.3 %copy-start.13 = (bf16[1,2,128,576]{3,2,1,0:T(8,128)(2,1)}, bf16[1,2,128,576]{3,2,1,0:T(8,128)(2,1)S(1)}, u32[]{:S(2)}) copy-start(bf16[1,2,128,576]{3,2,1,0:T(8,128)(2,1)S(1)} %copy.22) | copy-start | bytes 884740
  64.7 8.2 %copy-start.19 = (bf16[2,512,1]{2,1,0:T(8,128)(2,1)S(1)}, bf16[2,512,1]{2,1,0:T(8,128)(2,1)}, u32[]{:S(2)}) copy-start(bf16[2,512,1]{2,1,0:T(8,128)(2,1)} %select_convert_fusion) | copy-start | bytes 6148
  64.7 8.2 %copy-start.20 = (bf16[1024,128]{1,0:T(8,128)(2,1)S(1)}, bf16[1024,128]{1,0:T(8,128)(2,1)}, u32[]{:S(2)}) copy-start(bf16[1024,128]{1,0:T(8,128)(2,1)} %pad.31.clone) | copy-start | bytes 786436
  64.8 8.2 %copy-start.21 = (bf16[2,512,64]{2,1,0:T(8,128)(2,1)S(1)}, bf16[2,512,64]{2,1,0:T(8,128)(2,1)}, u32[]{:S(2)}) copy-start(bf16[2,512,64]{2,1,0:T(8,128)(2,1)} %broadcast_select_fusion) | copy-start | bytes 393220
  64.8 9.2 %copy-start.38 = (bf16[512,32,128]{2,1,0:T(8,128)(2,1)S(1)}, bf16[512,32,128]{2,1,0:T(8,128)(2,1)}, u32[]{:S(2)}) copy-start(bf16[512,32,128]{2,1,0:T(8,128)(2,1)} %param.27) | copy-start | bytes 12582916
  134.4 32.2 %collective-permute-start.8 = (f32[128,3584]{1,0:T(8,128)}, f32[128,3584]{1,0:T(8,128)S(1)}, u32[]{:S(2)}, u32[]{:S(2)}) collective-permute-start(f32[128,3584]{1,0:T(8,128)} %get-tuple-element.23), channel_id=1, source_target_pairs={{0,1},{1,0},{2,3},{3,2},{4,5},{5,4},{6,7},{7,6}} | collective-permute-start | bytes 5505032 | tf_op jit(solution)/shard_map/ppermute | solution.py:240
  157.7 9.0 %copy-start.18 = (f32[128,3584]{1,0:T(8,128)S(1)}, f32[128,3584]{1,0:T(8,128)}, u32[]{:S(2)}) copy-start(f32[128,3584]{1,0:T(8,128)} %get-tuple-element.22) | copy-start | bytes 5505028
  157.7 49.4 %collective-permute-start.9 = (f32[128,3584]{1,0:T(8,128)}, f32[128,3584]{1,0:T(8,128)}, u32[]{:S(2)}, u32[]{:S(2)}) collective-permute-start(f32[128,3584]{1,0:T(8,128)} %get-tuple-element.25), channel_id=1, source_target_pairs={{0,1},{1,0},{2,3},{3,2},{4,5},{5,4},{6,7},{7,6}} | collective-permute-start | bytes 5505032 | tf_op jit(solution)/shard_map/ppermute | solution.py:240
  168.1 39.0 %copy-start.17 = (f32[128,3584]{1,0:T(8,128)S(1)}, f32[128,3584]{1,0:T(8,128)}, u32[]{:S(2)}) copy-start(f32[128,3584]{1,0:T(8,128)} %get-tuple-element.21) | copy-start | bytes 5505028
  210.1 15.9 %copy-start.27 = (f32[128,32]{0,1:T(8,128)S(1)}, f32[128,32]{0,1:T(8,128)}, u32[]{:S(2)}) copy-start(f32[128,32]{0,1:T(8,128)} %get-tuple-element.91) | copy-start | bytes 49156
  210.1 15.9 %copy-start.28 = (f32[128,32]{0,1:T(8,128)S(1)}, f32[128,32]{0,1:T(8,128)}, u32[]{:S(2)}) copy-start(f32[128,32]{0,1:T(8,128)} %get-tuple-element.92) | copy-start | bytes 49156
  210.1 16.5 %copy-start.25 = (f32[128,32]{0,1:T(8,128)S(1)}, f32[128,32]{0,1:T(8,128)}, u32[]{:S(2)}) copy-start(f32[128,32]{0,1:T(8,128)} %get-tuple-element.73) | copy-start | bytes 49156
  210.1 16.5 %copy-start.26 = (f32[128,32]{0,1:T(8,128)S(1)}, f32[128,32]{0,1:T(8,128)}, u32[]{:S(2)}) copy-start(f32[128,32]{0,1:T(8,128)} %get-tuple-element.74) | copy-start | bytes 49156
  225.1 24.7 %collective-permute-start.10 = (f32[128,3584]{1,0:T(8,128)}, f32[128,3584]{1,0:T(8,128)}, u32[]{:S(2)}, u32[]{:S(2)}) collective-permute-start(f32[128,3584]{1,0:T(8,128)} %get-tuple-element.29), channel_id=1, source_target_pairs={{0,1},{1,0},{2,3},{3,2},{4,5},{5,4},{6,7},{7,6}} | collective-permute-start | bytes 5505032 | tf_op jit(solution)/shard_map/ppermute | solution.py:240
  225.5 20.2 %collective-permute-start = (bf16[128,1536]{1,0:T(8,128)(2,1)}, bf16[128,1536]{1,0:T(8,128)(2,1)}, u32[]{:S(2)}, u32[]{:S(2)}) collective-permute-start(bf16[128,1536]{1,0:T(8,128)(2,1)} %get-tuple-element.53), channel_id=1, source_target_pairs={{0,1},{1,0},{2,3},{3,2},{4,5},{5,4},{6,7},{7,6}} | collective-permute-start | bytes 1179656 | tf_op jit(solution)/shard_map/ppermute | solution.py:240
  225.6 22.2 %collective-permute-start.11 = (bf16[128,1536]{1,0:T(8,128)(2,1)S(1)}, bf16[128,1536]{1,0:T(8,128)(2,1)}, u32[]{:S(2)}, u32[]{:S(2)}) collective-permute-start(bf16[128,1536]{1,0:T(8,128)(2,1)S(1)} %get-tuple-element.54), channel_id=1, source_target_pairs={{0,1},{1,0},{2,3},{3,2},{4,5},{5,4},{6,7},{7,6}} | collective-permute-start | bytes 1179656 | tf_op jit(solution)/shard_map/ppermute | solution.py:240
  242.2 7.6 %copy-start.15 = (f32[128,3584]{1,0:T(8,128)S(1)}, f32[128,3584]{1,0:T(8,128)}, u32[]{:S(2)}) copy-start(f32[128,3584]{1,0:T(8,128)} %get-tuple-element.28) | copy-start | bytes 5505028
  242.2 47.1 %collective-permute-start.12 = (f32[128,3584]{1,0:T(8,128)}, f32[128,3584]{1,0:T(8,128)}, u32[]{:S(2)}, u32[]{:S(2)}) collective-permute-start(f32[128,3584]{1,0:T(8,128)} %get-tuple-element.31), channel_id=1, source_target_pairs={{0,1},{1,0},{2,3},{3,2},{4,5},{5,4},{6,7},{7,6}} | collective-permute-start | bytes 5505032 | tf_op jit(solution)/shard_map/ppermute | solution.py:240
  249.7 133.0 %collective-permute-start.17 = (f32[128,3584]{1,0:T(8,128)}, f32[128,3584]{1,0:T(8,128)}, u32[]{:S(2)}, u32[]{:S(2)}) collective-permute-start(f32[128,3584]{1,0:T(8,128)} %add.124), channel_id=1, source_target_pairs={{0,2},{1,3},{2,0},{3,1},{4,6},{5,7},{6,4},{7,5}} | collective-permute-start | bytes 5505032 | tf_op jit(solution)/shard_map/ppermute | solution.py:243
  252.7 36.6 %copy-start.16 = (f32[128,3584]{1,0:T(8,128)S(1)}, f32[128,3584]{1,0:T(8,128)}, u32[]{:S(2)}) copy-start(f32[128,3584]{1,0:T(8,128)} %get-tuple-element.27) | copy-start | bytes 5505028
  352.3 32.4 %copy-start.34 = (s32[2]{0:T(128)S(1)}, s32[2]{0:T(128)}, u32[]{:S(2)}) copy-start(s32[2]{0:T(128)} %param.16) | copy-start | bytes 28
  352.3 38.7 %copy-start.3 = (bf16[2,1024,512]{2,1,0:T(8,128)(2,1)S(1)}, bf16[2,1024,512]{2,1,0:T(8,128)(2,1)}, u32[]{:S(2)}) copy-start(bf16[2,1024,512]{2,1,0:T(8,128)(2,1)} %param.19) | copy-start | bytes 6291460
  375.8 126.2 %collective-permute-start.16 = (f32[256,3584]{1,0:T(8,128)}, f32[256,3584]{1,0:T(8,128)}, u32[]{:S(2)}, u32[]{:S(2)}) collective-permute-start(f32[256,3584]{1,0:T(8,128)} %get-tuple-element.38), channel_id=1, source_target_pairs={{0,1},{1,0},{2,3},{3,2},{4,5},{5,4},{6,7},{7,6}} | collective-permute-start | bytes 11010056 | tf_op jit(solution)/shard_map/ppermute | solution.py:240
  376.2 125.7 %collective-permute-start.13 = (f32[256,3584]{1,0:T(8,128)}, f32[256,3584]{1,0:T(8,128)}, u32[]{:S(2)}, u32[]{:S(2)}) collective-permute-start(f32[256,3584]{1,0:T(8,128)} %get-tuple-element.35), channel_id=1, source_target_pairs={{0,1},{1,0},{2,3},{3,2},{4,5},{5,4},{6,7},{7,6}} | collective-permute-start | bytes 11010056 | tf_op jit(solution)/shard_map/ppermute | solution.py:240
  376.3 47.5 %collective-permute-start.14 = (f32[128,3584]{1,0:T(8,128)}, f32[128,3584]{1,0:T(8,128)}, u32[]{:S(2)}, u32[]{:S(2)}) collective-permute-start(f32[128,3584]{1,0:T(8,128)} %add.123), channel_id=1, source_target_pairs={{0,2},{1,3},{2,0},{3,1},{4,6},{5,7},{6,4},{7,5}} | collective-permute-start | bytes 5505032 | tf_op jit(solution)/shard_map/ppermute | solution.py:243
  382.7 80.5 %collective-permute-start.18 = (f32[128,3584]{1,0:T(8,128)}, f32[128,3584]{1,0:T(8,128)}, u32[]{:S(2)}, u32[]{:S(2)}) collective-permute-start(f32[128,3584]{1,0:T(8,128)} %add.127), channel_id=1, source_target_pairs={{0,2},{1,3},{2,0},{3,1},{4,6},{5,7},{6,4},{7,5}} | collective-permute-start | bytes 5505032 | tf_op jit(solution)/shard_map/ppermute | solution.py:243
  382.7 119.2 %collective-permute-start.15 = (f32[128,3584]{1,0:T(8,128)}, f32[128,3584]{1,0:T(8,128)}, u32[]{:S(2)}, u32[]{:S(2)}) collective-permute-start(f32[128,3584]{1,0:T(8,128)} %add.125), channel_id=1, source_target_pairs={{0,2},{1,3},{2,0},{3,1},{4,6},{5,7},{6,4},{7,5}} | collective-permute-start | bytes 5505032 | tf_op jit(solution)/shard_map/ppermute | solution.py:243
  392.5 11.5 %copy-start.4 = (bf16[1,1024,512]{2,1,0:T(8,128)(2,1)S(1)}, bf16[1,1024,512]{2,1,0:T(8,128)(2,1)}, u32[]{:S(2)}) copy-start(bf16[1,1024,512]{2,1,0:T(8,128)(2,1)} %get-tuple-element.42) | copy-start | bytes 3145732
  397.4 10.4 %copy-start.22 = (bf16[1,1024,64]{1,2,0:T(8,128)(2,1)S(1)}, bf16[1,1024,64]{1,2,0:T(8,128)(2,1)}, u32[]{:S(2)}) copy-start(bf16[1,1024,64]{1,2,0:T(8,128)(2,1)} %dynamic_update_slice.18) | copy-start | bytes 393220
  407.8 94.1 %copy-start.1 = (bf16[2,128,7168]{2,1,0:T(8,128)(2,1)S(1)}, bf16[2,128,7168]{2,1,0:T(8,128)(2,1)}, u32[]{:S(2)}) copy-start(bf16[2,128,7168]{2,1,0:T(8,128)(2,1)} %param.15) | copy-start | bytes 11010052
  (11 other events, 47.1 us)

commit v2 on v0

--- a/solution.py
+++ b/solution.py
@@ -14,7 +14,8 @@
 LOG2E = 1.4426950408889634
 COL_TILE = 512
 COL_CHUNKS = 2
-HEADS_PER_STEP = 2
+HEADS_PER_STEP = 4
+W_SLOTS = 4
 
 
 def rms_norm(values, gain_vec):
@@ -127,32 +128,95 @@
     )(scal, q, k_old, k_new, v_old, v_new, r_cat, cos_tab, sin_tab)
 
 
-def out_proj_kernel(o_ref, w_ref, ya_ref, yb_ref):
-    half = ya_ref.shape[0]
-    prod = jnp.dot(o_ref[...], w_ref[...], preferred_element_type=F32)
-    ya_ref[...] = prod[:half]
-    yb_ref[...] = prod[half:]
-
-
-def out_proj(o, w_out, first, count):
-    m_rows, depth = o.shape
+def out_proj_kernel(*refs, n_in, first):
+    o_hbm = refs[:n_in]
+    w_hbm, near_ref, far_ref, o_buf, w_buf, o_sems, w_sems = refs[n_in:]
+    j = pl.program_id(0)
+    tiles = pl.num_programs(0)
+    slots = w_buf.shape[0]
+    half = o_buf.shape[1] // 2
+    depth = w_buf.shape[1]
+
+    def weights(tile, slot):
+        col = pl.multiple_of((tile + first) * COL_TILE, COL_TILE)
+        return pltpu.make_async_copy(w_hbm.at[:, pl.ds(col, COL_TILE)], w_buf.at[slot], w_sems.at[slot])
+
+    @pl.when(j == 0)
+    def _():
+        weights(0, 0).start()
+        loads = [pltpu.make_async_copy(o_hbm[i], o_buf.at[i, :, :depth], o_sems.at[i]) for i in range(n_in)]
+        for load in loads:
+            load.start()
+        for slot in range(1, slots):
+            weights(slot, slot).start()
+        for load in loads:
+            load.wait()
+
+    slot = lax.rem(j, slots)
+    weights(j, slot).wait()
+    for i in range(n_in):
+        prod = jnp.dot(o_buf[i, :, :depth], w_buf[slot], preferred_element_type=F32)
+        near_ref[i * half:(i + 1) * half, :] = prod[:half]
+        far_ref[i * half:(i + 1) * half, :] = prod[half:]
+
+    @pl.when(j + slots < tiles)
+    def _():
+        weights(j + slots, slot).start()
+
+
+def out_proj(o_list, w_out, first, count):
+    m_rows, depth = o_list[0].shape
+    n_in = len(o_list)
     half = m_rows // 2
     tiles = count // COL_TILE
-    off = first // COL_TILE
-    out = jax.ShapeDtypeStruct((half, count), F32)
+    out = jax.ShapeDtypeStruct((n_in * half, count), F32)
+    raw = pl.BlockSpec(memory_space=pl.ANY)
+    out_spec = pl.BlockSpec((n_in * half, COL_TILE), lambda j: (0, j))
     return pl.pallas_call(
-        out_proj_kernel,
+        functools.partial(out_proj_kernel, n_in=n_in, first=first // COL_TILE),
         out_shape=(out, out),
         grid=(tiles,),
-        in_specs=[
-            pl.BlockSpec((m_rows, depth), lambda j: (0, 0)),
-            pl.BlockSpec((depth, COL_TILE), lambda j: (0, j + off)),
+        in_specs=[raw] * (n_in + 1),
+        out_specs=(out_spec, out_spec),
+        scratch_shapes=[
+            pltpu.VMEM((n_in, m_rows, depth + 128), BF16),
+            pltpu.VMEM((W_SLOTS, depth, COL_TILE), BF16),
+            pltpu.SemaphoreType.DMA((n_in,)),
+            pltpu.SemaphoreType.DMA((W_SLOTS,)),
         ],
-        out_specs=(pl.BlockSpec((half, COL_TILE), lambda j: (0, j)), pl.BlockSpec((half, COL_TILE), lambda j: (0, j))),
         compiler_params=pltpu.CompilerParams(dimension_semantics=("arbitrary",)),
-        cost_estimate=pl.CostEstimate(flops=2 * m_rows * depth * count, bytes_accessed=depth * count * 2 + m_rows * count * 4, transcendentals=0),
+        cost_estimate=pl.CostEstimate(flops=2 * n_in * m_rows * depth * count, bytes_accessed=depth * count * 2 + n_in * m_rows * count * 4, transcendentals=0),
         name="out_proj",
-    )(o, w_out)
+    )(*o_list, w_out)
+
+
+def cache_kernel(len_ref, lat_ref, lat_new_ref, pe_ref, pe_new_ref, lat_out_ref, pe_out_ref):
+    start = len_ref[pl.program_id(0)]
+    for old_ref, new_ref, out_ref, axis in ((lat_ref, lat_new_ref, lat_out_ref, 0), (pe_ref, pe_new_ref, pe_out_ref, 1)):
+        new = new_ref[0].astype(F32)
+        count = new.shape[axis]
+        wide = jnp.concatenate([new, jnp.zeros_like(new)], axis=axis)
+        moved = pltpu.roll(wide, start, axis)
+        pos = lax.broadcasted_iota(jnp.int32, wide.shape, axis)
+        inside = jnp.logical_and(pos >= start, pos < start + count)
+        out_ref[0] = jnp.where(inside, moved, old_ref[0].astype(F32)).astype(BF16)
+
+
+def write_caches(lengths, lat, lat_new, pe_t, pe_new_t):
+    spec = lambda arr: pl.BlockSpec((1,) + arr.shape[1:], lambda b, s: (b, 0, 0))
+    return pl.pallas_call(
+        cache_kernel,
+        out_shape=(jax.ShapeDtypeStruct(lat.shape, lat.dtype), jax.ShapeDtypeStruct(pe_t.shape, pe_t.dtype)),
+        grid_spec=pltpu.PrefetchScalarGridSpec(
+            num_scalar_prefetch=1,
+            grid=(lat.shape[0],),
+            in_specs=[spec(lat), spec(lat_new), spec(pe_t), spec(pe_new_t)],
+            out_specs=(spec(lat), spec(pe_t)),
+        ),
+        compiler_params=pltpu.CompilerParams(dimension_semantics=("arbitrary",)),
+        cost_estimate=pl.CostEstimate(flops=20_000_000, bytes_accessed=2 * lat.size * 2, transcendentals=0),
+        name="write_caches",
+    )(lengths, lat, lat_new, pe_t, pe_new_t)
 
 
 def solution(mesh):
@@ -248,22 +312,25 @@
             for j in range(COL_CHUNKS):
                 if len(pending) > 1 - (j == 0):
                     o = after(o, send_one())
-                near_part, far_part = out_proj(o, w_out, j * width, width)
+                near_part, far_part = out_proj([o], w_out, j * width, width)
                 pending.append((b, j, near_part, partner(far_part)))
         q_lat = jnp.concatenate([q_rel[b][k] for b in range(n_seq) for k in (0, 1)], axis=0)
-        q_lat = after(q_lat, near_part)
-        q_own = queries(q_lat)
-        while pending:
-            q_own = after(q_own, send_one())
-        result = []
+        q_own = queries(after(q_lat, near_part))
+        dep = (send_one(),)
+        o_own = []
         for b in range(n_seq):
-            o = attend(0, b, q_own, b)
-            own_part, partner_part = out_proj(o, w_out, 0, model_dim)
-            base = own_part + partner(partner_part) + hidden[b].astype(F32)
-            result.append((base + jnp.concatenate(arrived[b], axis=1)).astype(BF16))
-        out = jnp.stack(result)
-        lat_all = jnp.stack([lax.dynamic_update_slice(cache_lat[b], lat_new[b], (lengths[b], 0)) for b in range(n_seq)])
-        pe_all = jnp.stack([lax.dynamic_update_slice(cache_pe[b], pe_new[b], (lengths[b], 0)) for b in range(n_seq)])
+            o_own.append(attend(0, b, after(q_own, *dep), b))
+            dep = (o_own[-1],) + ((send_one(),) if pending else ())
+        cols = []
+        flat = hidden.reshape(n_seq * n_tok, model_dim)
+        for j in range(COL_CHUNKS):
+            own_part, partner_part = out_proj([after(o_own[0], *dep), o_own[1]], w_out, j * width, width)
+            dep = (own_part,)
+            base = own_part + partner(partner_part) + flat[:, j * width:(j + 1) * width].astype(F32)
+            cols.append(base + jnp.concatenate([arrived[b][j] for b in range(n_seq)], axis=0))
+        out = jnp.concatenate(cols, axis=1).astype(BF16).reshape(hidden.shape)
+        lat_all, pe_all_t = write_caches(lengths, cache_lat, lat_new, cache_pe.transpose(0, 2, 1), pe_new.transpose(0, 2, 1))
+        pe_all = pe_all_t.transpose(0, 2, 1)
         return out, lat_all, pe_all
 
     spec_tok = P("dp", "tp", None)

time: 504 us -> 479 us (0.950)
  Pallas kernels: 218 us -> 195 us
  waiting for transfers between devices: 90.7 us -> 110 us
  local copies, waits for them, and re-layouts: 22.5 us -> 6.66 us
    ppermute x7, waiting for transfers between devices: 90.7 us -> 110 us  [other_chip(): return lax.ppermute(value, 'tp', to_chip)]
    pallas_call x4, Pallas kernels: 95.4 us -> 83.1 us  [attention(): pl.pallas_call(functools.partial(attention_kernel, scale=scale), out_shap...]
    dynamic_update_slice x4 -> x0, local copies, waits for them, and re-layouts: 11.2 us -> none  [the longest x2 7.79 us: step(): lax.dynamic_update_slice(cache_lat[b], lat_new[b], (lengths[b], 0))]
    pallas_call x6 -> x7, Pallas kernels: 123 us -> 112 us  [the longest x6 107 us: out_proj(): pl.pallas_call(functools.partial(out_proj_kernel, n_in=n_in, first=first...]
    slice x9 -> x3, local copies, waits for them, and re-layouts: 7.28 us -> 1.33 us  [step(): lat_new = kv_true[..., :kv_rank]]
    another operation x5 -> x2, other arithmetic: 14.6 us -> 9.66 us  [the longest x2 10.6 us: step(): out = jnp.stack(result)]
  transfers between devices with their start and end apart: 19 -> 19, of which waited for: 3 -> 3; matrix products, arithmetic and copies ran while one was open for 29% -> 25% of each run, Pallas kernels for 44% -> 38%
where the time goes in v2:
time: 479 us; the launch traced here: 474 us
  Pallas kernels  195 us (41%)
  waiting for transfers between devices  110 us (23%)
  matrix products  106 us (22%)
  other arithmetic  40.4 us (8%)
  starting transfers between devices  14.3 us (3%)
  local copies, waits for them, and re-layouts  6.66 us (1%)
    ppermute x7, waiting for transfers between devices, other_chip(): return lax.ppermute(value, 'tp', to_chip)  110 us
    pallas_call x6, Pallas kernels, out_proj(): pl.pallas_call(functools.partial(out_proj_kernel, n_in=n_in, first=first...  107 us
    pallas_call x4, Pallas kernels, attention(): pl.pallas_call(functools.partial(attention_kernel, scale=scale), out_shap...  83.1 us
    unnamed x3, matrix products  40.3 us
    dot_general x4, matrix products, project(): jnp.einsum('chv,sc->hvs', w_uv, lat, preferred_element_type=F32)  26.1 us
    dot_general x4, matrix products, project(): jnp.einsum('sc,chd->hsd', lat, w_uk, preferred_element_type=F32)  21 us
    dot_general x1, matrix products, step(): jnp.dot(normed, w_dq, preferred_element_type=F32)  11.7 us
    ppermute x7, starting transfers between devices, other_chip(): return lax.ppermute(value, 'tp', to_chip)  11.2 us
  transfers between devices with their start and end apart: 19, of which 3 were waited for; matrix products, arithmetic and copies ran while one was open for 25% of the time, Pallas kernels for 38%

profile of v2, /device:TPU:0, one launch (start us, length us, event | category | flops | bytes accessed | tf_op | source)
XLA Modules:
  0.0 474.0 jit_solution(2979932334455236469)
XLA Ops:
  0.6 3.0 fusion.2
  3.8 1.8 fusion.4
  5.6 11.7 %multiply_reduce_fusion = (f32[256]{0:T(256)S(1)}, f32[256,1536]{1,0:T(8,128)S(1)}) fusion(bf16[256,7168]{1,0:T(8,128)(2,1)S(1)} %bitcast.148, bf16[7168,1536]{1,0:T(8,128)(2,1)} %param.22), kind=kOutput, calls=%fused_computation.38 | convolution fusion | flops 5637931008 | bytes 27264000 | tf_op jit(solution)/shard_map/dot_general | solution.py:250
  17.6 3.3 collective-permute-start.4
  21.4 6.5 %fusion = f32[2,128,576]{1,2,0:T(8,128)S(1)} fusion(bf16[2,128,7168]{2,1,0:T(8,128)(2,1)} %copy-done.3, bf16[7168,576]{0,1:T(8,128)(2,1)} %param.24), kind=kOutput, calls=%fused_computation.2 | convolution fusion | flops 2113929216 | bytes 12517376 | tf_op jit(solution)/shard_map/dot_general | solution.py:244
  28.2 0.8 subtract_convert_fusion
  29.8 1.7 collective-permute-start.7
  31.5 0.9 fusion.49
  32.4 0.9 fusion.50
  33.6 8.0 %convert_bitcast_fusion.5.v_old_ref = bf16[32,128,512]{2,1,0:T(8,128)(2,1)} fusion(bf16[512,32,128]{2,1,0:T(8,128)(2,1)} %param.28, bf16[2,512,512]{2,1,0:T(8,128)(2,1)S(1)} %slice_select_fusion), kind=kOutput, calls=%fused_computation.12 | convolution fusion | flops 2149580800 | bytes 8912896 | tf_op jit(solution)/shard_map/chv,sc->hvs/dot_general | solution.py:265
  41.6 6.0 %convert_bitcast_fusion.1.v_old_ref = bf16[32,128,512]{2,1,0:T(8,128)(2,1)} fusion(bf16[512,32,128]{2,1,0:T(8,128)(2,1)S(1)} %copy-done.12, bf16[2,512,512]{2,1,0:T(8,128)(2,1)S(1)} %slice_select_fusion), kind=kOutput, calls=%fused_computation.8 | convolution fusion | flops 2149580800 | bytes 8912896 | tf_op jit(solution)/shard_map/chv,sc->hvs/dot_general | solution.py:265
  47.6 4.6 convert_bitcast_fusion.7.k_old_ref
  52.2 4.7 convert_bitcast_fusion.3.k_old_ref
  64.2 2.4 pad_maximum_fusion.1
  66.6 1.3 pad_maximum_fusion.2
  68.8 6.1 %convert_bitcast_fusion.4.v_new_ref = bf16[32,128,512]{2,1,0:T(8,128)(2,1)} fusion(bf16[512,32,128]{2,1,0:T(8,128)(2,1)S(1)} %copy-done.13, bf16[2,512,576]{1,2,0:T(8,128)(2,1)S(1)} %pad_maximum_fusion.3), kind=kOutput, calls=%fused_computation.11 | convolution fusion | flops 2149580800 | bytes 8912896 | tf_op jit(solution)/shard_map/chv,sc->hvs/dot_general | solution.py:265
  74.9 4.9 %convert_bitcast_fusion.6.k_new_ref = bf16[32,512,128]{2,1,0:T(8,128)(2,1)} fusion(bf16[512,32,128]{2,1,0:T(8,128)(2,1)S(1)} %copy-done.15, bf16[2,512,576]{1,2,0:T(8,128)(2,1)S(1)} %pad_maximum_fusion.3), kind=kOutput, calls=%fused_computation.13 | convolution fusion | flops 2149580800 | bytes 8912896 | tf_op jit(solution)/shard_map/sc,chd->hsd/dot_general | solution.py:264
  79.8 6.0 %convert_bitcast_fusion.v_new_ref = bf16[32,128,512]{2,1,0:T(8,128)(2,1)} fusion(bf16[512,32,128]{2,1,0:T(8,128)(2,1)S(1)} %copy-done.13, bf16[2,512,576]{1,2,0:T(8,128)(2,1)S(1)} %pad_maximum_fusion.3), kind=kOutput, calls=%fused_computation.7 | convolution fusion | flops 2149580800 | bytes 8912896 | tf_op jit(solution)/shard_map/chv,sc->hvs/dot_general | solution.py:265
  86.5 1.0 copy.26.r_ref
  87.6 0.8 copy.35.r_ref
  88.4 6.8 %convert_bitcast_fusion.2.k_new_ref = bf16[32,512,128]{2,1,0:T(8,128)(2,1)} fusion(bf16[512,32,128]{2,1,0:T(8,128)(2,1)} %param.27, bf16[2,512,576]{1,2,0:T(8,128)(2,1)S(1)} %pad_maximum_fusion.3), kind=kOutput, calls=%fused_computation.9 | convolution fusion | flops 2149580800 | bytes 8912896 | tf_op jit(solution)/shard_map/sc,chd->hsd/dot_general | solution.py:264
  95.3 10.8 %fusion.40 = f32[256,6144]{0,1} fusion(bf16[1536,6144]{0,1:T(8,128)(2,1)} %bitcast.153, bf16[128,1536]{1,0:T(8,128)(2,1)S(1)} %collective-permute-done.5, bf16[128,1536]{1,0:T(8,128)(2,1)} %collective-permute-done.4), kind=kOutput, calls=%fused_computation.45 | convolution fusion | flops 4833411072 | bytes 25952256
  106.1 21.1 %attention.4.refs_0_ = bf16[256,4096]{1,0:T(8,128)(2,1)} custom-call(s32[3]{0:T(128)} %pad_add_fusion.1.scal_ref, f32[32,192,256]{2,1,0:T(8,128)} %bitcast.147, bf16[32,512,128]{2,1,0:T(8,128)(2,1)} %convert_bitcast_fusion.7.k_old_ref, bf16[32,512,128]{2,1,0:T(8,128)(2,1)} %convert_bitcast_fusion.6.k_new_ref, ...), custom_call_target="tpu_custom_call" | custom-call | flops 6442450944 | bytes 30000000 | tf_op jit(solution)/shard_map/attention/pallas_call | solution.py:107
  127.2 14.9 %out_proj.7 = (f32[128,3584]{1,0:T(8,128)}, f32[128,3584]{1,0:T(8,128)}) custom-call(bf16[256,4096]{1,0:T(8,128)(2,1)} %attention.4.refs_0_, bf16[4096,7168]{1,0:T(8,128)(2,1)} %refs_2_.3), custom_call_target="tpu_custom_call" | custom-call | flops 7516192768 | bytes 33030144 | tf_op jit(solution)/shard_map/out_proj/pallas_call | solution.py:175
  142.2 15.0 %out_proj.6 = (f32[128,3584]{1,0:T(8,128)}, f32[128,3584]{1,0:T(8,128)}) custom-call(bf16[256,4096]{1,0:T(8,128)(2,1)} %attention.4.refs_0_, bf16[4096,7168]{1,0:T(8,128)(2,1)} %refs_2_.3), custom_call_target="tpu_custom_call" | custom-call | flops 7516192768 | bytes 33030144 | tf_op jit(solution)/shard_map/out_proj/pallas_call | solution.py:175
  157.7 1.2 pad_maximum_fusion.4
  158.9 12.2 %fusion.51 = f32[256,6144]{0,1} fusion(bf16[256,1536]{1,0:T(8,128)(2,1)S(1)} %pad_maximum_fusion.4, bf16[1536,6144]{0,1:T(8,128)(2,1)} %bitcast.154), kind=kOutput, calls=%fused_computation.104 | convolution fusion | flops 4831838208 | bytes 25952256
  171.1 1.5 add.115
  172.6 21.4 %attention.5.refs_0_ = bf16[256,4096]{1,0:T(8,128)(2,1)} custom-call(s32[3]{0:T(128)} %pad_add_fusion.1.scal_ref, f32[32,192,256]{2,1,0:T(8,128)} %bitcast.146, bf16[32,512,128]{2,1,0:T(8,128)(2,1)} %convert_bitcast_fusion.3.k_old_ref, bf16[32,512,128]{2,1,0:T(8,128)(2,1)} %convert_bitcast_fusion.2.k_new_ref, ...), custom_call_target="tpu_custom_call" | custom-call | flops 6442450944 | bytes 30000000 | tf_op jit(solution)/shard_map/attention/pallas_call | solution.py:107
  194.0 2.9 add.116
  197.0 14.9 %out_proj.9 = (f32[128,3584]{1,0:T(8,128)}, f32[128,3584]{1,0:T(8,128)}) custom-call(bf16[256,4096]{1,0:T(8,128)(2,1)} %attention.5.refs_0_, bf16[4096,7168]{1,0:T(8,128)(2,1)} %refs_2_.3), custom_call_target="tpu_custom_call" | custom-call | flops 7516192768 | bytes 33030144 | tf_op jit(solution)/shard_map/out_proj/pallas_call | solution.py:175
  212.0 15.0 %out_proj.8 = (f32[128,3584]{1,0:T(8,128)}, f32[128,3584]{1,0:T(8,128)}) custom-call(bf16[256,4096]{1,0:T(8,128)(2,1)} %attention.5.refs_0_, bf16[4096,7168]{1,0:T(8,128)(2,1)} %refs_2_.3), custom_call_target="tpu_custom_call" | custom-call | flops 7516192768 | bytes 33030144 | tf_op jit(solution)/shard_map/out_proj/pallas_call | solution.py:175
  227.5 17.2 %fusion.52 = f32[512,6144]{0,1} fusion(bf16[512,1536]{1,0:T(8,128)(2,1)} %pad_maximum_fusion.1, bf16[1536,6144]{0,1:T(8,128)(2,1)} %bitcast.155), kind=kOutput, calls=%fused_computation.105 | convolution fusion | flops 9663676416 | bytes 33030144
  244.7 3.0 add.117
  247.7 20.0 %attention.6.refs_0_ = bf16[256,4096]{1,0:T(8,128)(2,1)} custom-call(s32[3]{0:T(128)} %pad_add_fusion.scal_ref, f32[32,192,512]{2,1,0:T(8,128)} %bitcast.141, bf16[32,512,128]{2,1,0:T(8,128)(2,1)} %convert_bitcast_fusion.7.k_old_ref, bf16[32,512,128]{2,1,0:T(8,128)(2,1)} %convert_bitcast_fusion.6.k_new_ref, ...), custom_call_target="tpu_custom_call" | custom-call | flops 6442450944 | bytes 30000000 | tf_op jit(solution)/shard_map/attention/pallas_call | solution.py:107
  267.7 3.6 add.119
  271.3 20.5 %attention.7.refs_1_ = bf16[256,4096]{1,0:T(8,128)(2,1)} custom-call(s32[3]{0:T(128)} %pad_add_fusion.scal_ref, f32[32,192,512]{2,1,0:T(8,128)} %bitcast.142, bf16[32,512,128]{2,1,0:T(8,128)(2,1)} %convert_bitcast_fusion.3.k_old_ref, bf16[32,512,128]{2,1,0:T(8,128)(2,1)} %convert_bitcast_fusion.2.k_new_ref, ...), custom_call_target="tpu_custom_call" | custom-call | flops 6442450944 | bytes 30000000 | tf_op jit(solution)/shard_map/attention/pallas_call | solution.py:107
  291.8 23.4 %out_proj.10 = (f32[256,3584]{1,0:T(8,128)}, f32[256,3584]{1,0:T(8,128)}) custom-call(bf16[256,4096]{1,0:T(8,128)(2,1)} %attention.6.refs_0_, bf16[256,4096]{1,0:T(8,128)(2,1)} %attention.7.refs_1_, bf16[4096,7168]{1,0:T(8,128)(2,1)} %refs_2_.3), custom_call_target="tpu_custom_call" | custom-call | flops 15032385536 | bytes 36700160 | tf_op jit(solution)/shard_map/out_proj/pallas_call | solution.py:175
  315.2 23.4 %out_proj.11 = (f32[256,3584]{1,0:T(8,128)}, f32[256,3584]{1,0:T(8,128)}) custom-call(bf16[256,4096]{1,0:T(8,128)(2,1)} %attention.6.refs_0_, bf16[256,4096]{1,0:T(8,128)(2,1)} %attention.7.refs_1_, bf16[4096,7168]{1,0:T(8,128)(2,1)} %refs_2_.3), custom_call_target="tpu_custom_call" | custom-call | flops 15032385536 | bytes 36700160 | tf_op jit(solution)/shard_map/out_proj/pallas_call | solution.py:175
  339.1 4.0 collective-permute-start.14
  343.2 2.0 collective-permute-start.15
  345.2 1.3 copy.38.lat_new_ref
  346.5 5.8 %write_caches.1 = (bf16[2,1024,512]{2,1,0:T(8,128)(2,1)}, bf16[2,64,1024]{2,1,0:T(8,128)(2,1)}) custom-call(s32[2]{0:T(128)} %len_ref.1, bf16[2,1024,512]{2,1,0:T(8,128)(2,1)} %lat_ref.1, bf16[2,512,512]{2,1,0:T(8,128)(2,1)} %copy.38.lat_new_ref, bf16[2,64,1024]{2,1,0:T(8,128)(2,1)} %bitcast.150, bf16[2,64,512]{2,1,0:T(8,128)(2,1)} %bitcast.149), custom_call_target="tpu_custom_call" | custom-call | flops 20000000 | bytes 4194304 | tf_op jit(solution)/shard_map/write_caches/pallas_call | solution.py:207
  352.3 32.0 %collective-permute-done.14 = f32[128,3584]{1,0:T(8,128)} collective-permute-done((f32[128,3584]{1,0:T(8,128)}, f32[128,3584]{1,0:T(8,128)}, u32[]{:S(2)}, u32[]{:S(2)}) %collective-permute-start.14) | collective-permute-done | bytes 1835040 | tf_op jit(solution)/shard_map/ppermute | solution.py:231
  384.3 39.3 %collective-permute-done.18 = f32[128,3584]{1,0:T(8,128)} collective-permute-done((f32[128,3584]{1,0:T(8,128)}, f32[128,3584]{1,0:T(8,128)}, u32[]{:S(2)}, u32[]{:S(2)}) %collective-permute-start.18) | collective-permute-done | bytes 1835040 | tf_op jit(solution)/shard_map/ppermute | solution.py:231
  423.6 39.0 %collective-permute-done.15 = f32[128,3584]{1,0:T(8,128)} collective-permute-done((f32[128,3584]{1,0:T(8,128)}, f32[128,3584]{1,0:T(8,128)}, u32[]{:S(2)}, u32[]{:S(2)}) %collective-permute-start.15) | collective-permute-done | bytes 1835040 | tf_op jit(solution)/shard_map/ppermute | solution.py:231
  462.6 8.9 %fusion.5 = (bf16[256,3584]{1,0:T(8,128)(2,1)S(1)}, bf16[256,3584]{1,0:T(8,128)(2,1)S(1)}) fusion(f32[128,3584]{1,0:T(8,128)} %collective-permute-done.15, f32[128,3584]{1,0:T(8,128)} %collective-permute-done.14, f32[256,3584]{1,0:T(8,128)} %get-tuple-element.40, f32[256,3584]{1,0:T(8,128)} %collective-permute-done.13, bf16[256,7168]{1,0:T(8,128)(2,1)} %bitcast.143, ...), kind=kLoop, calls=%fused_computation.16 | loop fusion | flops 11010048 | bytes 29360128 | tf_op jit(solution)/shard_map/convert.3
  471.5 2.3 pad_maximum_fusion
  (95 shorter events, 12.9 us)
Async XLA Ops:
  0.6 3.1 copy-start
  5.6 11.7 %copy-start.3 = (bf16[2,128,7168]{2,1,0:T(8,128)(2,1)}, bf16[2,128,7168]{2,1,0:T(8,128)(2,1)S(1)}, u32[]{:S(2)}) copy-start(bf16[2,128,7168]{2,1,0:T(8,128)(2,1)S(1)} %fusion.4) | copy-start | bytes 11010052
  5.6 11.7 %copy-start.9 = (f32[1536]{0:T(1024)S(1)}, f32[1536]{0:T(1024)}, u32[]{:S(2)}) copy-start(f32[1536]{0:T(1024)} %param.23) | copy-start | bytes 18436
  17.6 44.8 %collective-permute-start.4 = (bf16[128,1536]{1,0:T(8,128)(2,1)S(1)}, bf16[128,1536]{1,0:T(8,128)(2,1)}, u32[]{:S(2)}, u32[]{:S(2)}) collective-permute-start(bf16[128,1536]{1,0:T(8,128)(2,1)S(1)} %get-tuple-element.55), channel_id=1, source_target_pairs={{0,2},{1,3},{2,0},{3,1},{4,6},{5,7},{6,4},{7,5}} | collective-permute-start | bytes 1179656 | tf_op jit(solution)/shard_map/ppermute | solution.py:231
  20.9 42.8 %collective-permute-start = (bf16[128,1536]{1,0:T(8,128)(2,1)S(1)}, bf16[128,1536]{1,0:T(8,128)(2,1)}, u32[]{:S(2)}, u32[]{:S(2)}) collective-permute-start(bf16[128,1536]{1,0:T(8,128)(2,1)S(1)} %get-tuple-element.55), channel_id=1, source_target_pairs={{0,1},{1,0},{2,3},{3,2},{4,5},{5,4},{6,7},{7,6}} | collective-permute-start | bytes 1179656 | tf_op jit(solution)/shard_map/ppermute | solution.py:228
  20.9 42.7 %collective-permute-start.2 = (bf16[128,1536]{1,0:T(8,128)(2,1)S(1)}, bf16[128,1536]{1,0:T(8,128)(2,1)}, u32[]{:S(2)}, u32[]{:S(2)}) collective-permute-start(bf16[128,1536]{1,0:T(8,128)(2,1)S(1)} %get-tuple-element.56), channel_id=1, source_target_pairs={{0,2},{1,3},{2,0},{3,1},{4,6},{5,7},{6,4},{7,5}} | collective-permute-start | bytes 1179656 | tf_op jit(solution)/shard_map/ppermute | solution.py:231
  21.0 43.2 %collective-permute-start.1 = (bf16[128,1536]{1,0:T(8,128)(2,1)S(1)}, bf16[128,1536]{1,0:T(8,128)(2,1)}, u32[]{:S(2)}, u32[]{:S(2)}) collective-permute-start(bf16[128,1536]{1,0:T(8,128)(2,1)S(1)} %get-tuple-element.56), channel_id=1, source_target_pairs={{0,1},{1,0},{2,3},{3,2},{4,5},{5,4},{6,7},{7,6}} | collective-permute-start | bytes 1179656 | tf_op jit(solution)/shard_map/ppermute | solution.py:228
  21.4 6.6 %copy-start.11 = (f32[512]{0:T(512)S(1)}, f32[512]{0:T(512)}, u32[]{:S(2)}) copy-start(f32[512]{0:T(512)} %param.25) | copy-start | bytes 6148
  21.4 11.8 %copy-start.10 = (s32[2]{0:T(128)S(1)}, s32[2]{0:T(128)}, u32[]{:S(2)}) copy-start(s32[2]{0:T(128)} %len_ref.1) | copy-start | bytes 28
  21.4 11.9 %copy-start.1 = (bf16[2,1024,512]{2,1,0:T(8,128)(2,1)S(1)}, bf16[2,1024,512]{2,1,0:T(8,128)(2,1)}, u32[]{:S(2)}) copy-start(bf16[2,1024,512]{2,1,0:T(8,128)(2,1)} %lat_ref.1) | copy-start | bytes 6291460
  29.8 32.6 %collective-permute-start.7 = (bf16[2,128,576]{1,2,0:T(8,128)(2,1)}, bf16[2,128,576]{1,2,0:T(8,128)(2,1)}, u32[]{:S(2)}, u32[]{:S(2)}) collective-permute-start(bf16[2,128,576]{1,2,0:T(8,128)(2,1)} %get-tuple-element.60), channel_id=1, source_target_pairs={{0,2},{1,3},{2,0},{3,1},{4,6},{5,7},{6,4},{7,5}} | collective-permute-start | bytes 884744 | tf_op jit(solution)/shard_map/ppermute | solution.py:231
  33.6 8.0 %copy-start.12 = (bf16[512,32,128]{2,1,0:T(8,128)(2,1)S(1)}, bf16[512,32,128]{2,1,0:T(8,128)(2,1)}, u32[]{:S(2)}) copy-start(bf16[512,32,128]{2,1,0:T(8,128)(2,1)} %param.28) | copy-start | bytes 12582916
  41.6 6.0 %copy-start.14 = (bf16[512,32,128]{2,1,0:T(8,128)(2,1)S(1)}, bf16[512,32,128]{2,1,0:T(8,128)(2,1)}, u32[]{:S(2)}) copy-start(bf16[512,32,128]{2,1,0:T(8,128)(2,1)} %param.27) | copy-start | bytes 12582916
  62.4 4.2 collective-permute-start.6
  62.4 4.1 collective-permute-start.8
  63.6 31.6 %collective-permute-start.5 = (bf16[128,1536]{1,0:T(8,128)(2,1)}, bf16[128,1536]{1,0:T(8,128)(2,1)S(1)}, u32[]{:S(2)}, u32[]{:S(2)}) collective-permute-start(bf16[128,1536]{1,0:T(8,128)(2,1)} %collective-permute-done.4), channel_id=1, source_target_pairs={{0,1},{1,0},{2,3},{3,2},{4,5},{5,4},{6,7},{7,6}} | collective-permute-start | bytes 1179656 | tf_op jit(solution)/shard_map/ppermute | solution.py:228
  63.7 94.0 %collective-permute-start.3 = (bf16[128,1536]{1,0:T(8,128)(2,1)}, bf16[128,1536]{1,0:T(8,128)(2,1)}, u32[]{:S(2)}, u32[]{:S(2)}) collective-permute-start(bf16[128,1536]{1,0:T(8,128)(2,1)} %collective-permute-done.2), channel_id=1, source_target_pairs={{0,1},{1,0},{2,3},{3,2},{4,5},{5,4},{6,7},{7,6}} | collective-permute-start | bytes 1179656 | tf_op jit(solution)/shard_map/ppermute | solution.py:228
  66.6 2.3 copy-start.13
  68.8 19.6 %copy-start.2 = (bf16[2,512,576]{1,2,0:T(8,128)(2,1)}, bf16[2,512,576]{1,2,0:T(8,128)(2,1)S(1)}, u32[]{:S(2)}) copy-start(bf16[2,512,576]{1,2,0:T(8,128)(2,1)S(1)} %pad_maximum_fusion.3) | copy-start | bytes 3538948
  68.8 6.1 %copy-start.15 = (bf16[512,32,128]{2,1,0:T(8,128)(2,1)S(1)}, bf16[512,32,128]{2,1,0:T(8,128)(2,1)}, u32[]{:S(2)}) copy-start(bf16[512,32,128]{2,1,0:T(8,128)(2,1)} %param.27) | copy-start | bytes 12582916
  79.8 6.0 %copy-start.8 = (bf16[2,1024,64]{1,2,0:T(8,128)(2,1)S(1)}, bf16[2,1024,64]{1,2,0:T(8,128)(2,1)}, u32[]{:S(2)}) copy-start(bf16[2,1024,64]{1,2,0:T(8,128)(2,1)} %param.20) | copy-start | bytes 786436
  85.9 0.6 copy-start.7
  142.2 29.0 %collective-permute-start.9 = (f32[128,3584]{1,0:T(8,128)}, f32[128,3584]{1,0:T(8,128)S(1)}, u32[]{:S(2)}, u32[]{:S(2)}) collective-permute-start(f32[128,3584]{1,0:T(8,128)} %get-tuple-element.28), channel_id=1, source_target_pairs={{0,1},{1,0},{2,3},{3,2},{4,5},{5,4},{6,7},{7,6}} | collective-permute-start | bytes 5505032 | tf_op jit(solution)/shard_map/ppermute | solution.py:228
  157.2 36.8 %collective-permute-start.10 = (f32[128,3584]{1,0:T(8,128)}, f32[128,3584]{1,0:T(8,128)}, u32[]{:S(2)}, u32[]{:S(2)}) collective-permute-start(f32[128,3584]{1,0:T(8,128)} %get-tuple-element.30), channel_id=1, source_target_pairs={{0,1},{1,0},{2,3},{3,2},{4,5},{5,4},{6,7},{7,6}} | collective-permute-start | bytes 5505032 | tf_op jit(solution)/shard_map/ppermute | solution.py:228
  158.9 12.3 %copy-start.5 = (f32[128,3584]{1,0:T(8,128)S(1)}, f32[128,3584]{1,0:T(8,128)}, u32[]{:S(2)}) copy-start(f32[128,3584]{1,0:T(8,128)} %get-tuple-element.27) | copy-start | bytes 5505028
  172.6 21.4 %copy-start.4 = (f32[128,3584]{1,0:T(8,128)S(1)}, f32[128,3584]{1,0:T(8,128)}, u32[]{:S(2)}) copy-start(f32[128,3584]{1,0:T(8,128)} %get-tuple-element.25) | copy-start | bytes 5505028
  211.9 32.8 %collective-permute-start.11 = (f32[128,3584]{1,0:T(8,128)}, f32[128,3584]{1,0:T(8,128)}, u32[]{:S(2)}, u32[]{:S(2)}) collective-permute-start(f32[128,3584]{1,0:T(8,128)} %get-tuple-element.35), channel_id=1, source_target_pairs={{0,1},{1,0},{2,3},{3,2},{4,5},{5,4},{6,7},{7,6}} | collective-permute-start | bytes 5505032 | tf_op jit(solution)/shard_map/ppermute | solution.py:228
  226.9 116.2 %collective-permute-start.17 = (f32[128,3584]{1,0:T(8,128)}, f32[128,3584]{1,0:T(8,128)S(1)}, u32[]{:S(2)}, u32[]{:S(2)}) collective-permute-start(f32[128,3584]{1,0:T(8,128)} %add.116), channel_id=1, source_target_pairs={{0,2},{1,3},{2,0},{3,1},{4,6},{5,7},{6,4},{7,5}} | collective-permute-start | bytes 5505032 | tf_op jit(solution)/shard_map/ppermute | solution.py:231
  227.0 40.8 %collective-permute-start.12 = (f32[128,3584]{1,0:T(8,128)}, f32[128,3584]{1,0:T(8,128)}, u32[]{:S(2)}, u32[]{:S(2)}) collective-permute-start(f32[128,3584]{1,0:T(8,128)} %get-tuple-element.37), channel_id=1, source_target_pairs={{0,1},{1,0},{2,3},{3,2},{4,5},{5,4},{6,7},{7,6}} | collective-permute-start | bytes 5505032 | tf_op jit(solution)/shard_map/ppermute | solution.py:228
  227.5 17.3 %copy-start.6 = (f32[128,3584]{1,0:T(8,128)S(1)}, f32[128,3584]{1,0:T(8,128)}, u32[]{:S(2)}) copy-start(f32[128,3584]{1,0:T(8,128)} %get-tuple-element.34) | copy-start | bytes 5505028
  315.2 30.0 %slice-start = ((bf16[2,512,576]{1,2,0:T(8,128)(2,1)}), bf16[2,512,512]{1,2,0:T(8,128)(2,1)S(1)}, s32[]{:S(2)}) async-start(bf16[2,512,576]{1,2,0:T(8,128)(2,1)} %copy-done.2), calls=%async_computation | async-start | bytes 2097152 | tf_op jit(solution)/shard_map/slice | solution.py:259
  338.6 124.0 %collective-permute-start.16 = (f32[256,3584]{1,0:T(8,128)}, f32[256,3584]{1,0:T(8,128)}, u32[]{:S(2)}, u32[]{:S(2)}) collective-permute-start(f32[256,3584]{1,0:T(8,128)} %get-tuple-element.44), channel_id=1, source_target_pairs={{0,1},{1,0},{2,3},{3,2},{4,5},{5,4},{6,7},{7,6}} | collective-permute-start | bytes 11010056 | tf_op jit(solution)/shard_map/ppermute | solution.py:228
  338.7 123.9 %collective-permute-start.13 = (f32[256,3584]{1,0:T(8,128)}, f32[256,3584]{1,0:T(8,128)}, u32[]{:S(2)}, u32[]{:S(2)}) collective-permute-start(f32[256,3584]{1,0:T(8,128)} %get-tuple-element.41), channel_id=1, source_target_pairs={{0,1},{1,0},{2,3},{3,2},{4,5},{5,4},{6,7},{7,6}} | collective-permute-start | bytes 11010056 | tf_op jit(solution)/shard_map/ppermute | solution.py:228
  339.1 45.2 %collective-permute-start.14 = (f32[128,3584]{1,0:T(8,128)}, f32[128,3584]{1,0:T(8,128)}, u32[]{:S(2)}, u32[]{:S(2)}) collective-permute-start(f32[128,3584]{1,0:T(8,128)} %add.115), channel_id=1, source_target_pairs={{0,2},{1,3},{2,0},{3,1},{4,6},{5,7},{6,4},{7,5}} | collective-permute-start | bytes 5505032 | tf_op jit(solution)/shard_map/ppermute | solution.py:231
  343.1 80.5 %collective-permute-start.18 = (f32[128,3584]{1,0:T(8,128)}, f32[128,3584]{1,0:T(8,128)}, u32[]{:S(2)}, u32[]{:S(2)}) collective-permute-start(f32[128,3584]{1,0:T(8,128)} %add.119), channel_id=1, source_target_pairs={{0,2},{1,3},{2,0},{3,1},{4,6},{5,7},{6,4},{7,5}} | collective-permute-start | bytes 5505032 | tf_op jit(solution)/shard_map/ppermute | solution.py:231
  343.2 119.4 %collective-permute-start.15 = (f32[128,3584]{1,0:T(8,128)}, f32[128,3584]{1,0:T(8,128)}, u32[]{:S(2)}, u32[]{:S(2)}) collective-permute-start(f32[128,3584]{1,0:T(8,128)} %add.117), channel_id=1, source_target_pairs={{0,2},{1,3},{2,0},{3,1},{4,6},{5,7},{6,4},{7,5}} | collective-permute-start | bytes 5505032 | tf_op jit(solution)/shard_map/ppermute | solution.py:231

commit v3 on v2

--- a/solution.py
+++ b/solution.py
@@ -13,7 +13,8 @@
 NEG = -1e30
 LOG2E = 1.4426950408889634
 COL_TILE = 512
-COL_CHUNKS = 2
+FAR_WIDTHS = (1536, 2560, 3072)
+OWN_WIDTHS = (4096, 3072)
 HEADS_PER_STEP = 4
 W_SLOTS = 4
 
@@ -134,8 +135,8 @@
     j = pl.program_id(0)
     tiles = pl.num_programs(0)
     slots = w_buf.shape[0]
-    half = o_buf.shape[1] // 2
-    depth = w_buf.shape[1]
+    m_rows = o_buf.shape[0] // n_in
+    half = m_rows // 2
 
     def weights(tile, slot):
         col = pl.multiple_of((tile + first) * COL_TILE, COL_TILE)
@@ -144,7 +145,7 @@
     @pl.when(j == 0)
     def _():
         weights(0, 0).start()
-        loads = [pltpu.make_async_copy(o_hbm[i], o_buf.at[i, :, :depth], o_sems.at[i]) for i in range(n_in)]
+        loads = [pltpu.make_async_copy(o_hbm[i], o_buf.at[pl.ds(i * m_rows, m_rows)], o_sems.at[i]) for i in range(n_in)]
         for load in loads:
             load.start()
         for slot in range(1, slots):
@@ -154,10 +155,10 @@
 
     slot = lax.rem(j, slots)
     weights(j, slot).wait()
+    prod = jnp.dot(o_buf[:, :], w_buf[slot], preferred_element_type=F32)
     for i in range(n_in):
-        prod = jnp.dot(o_buf[i, :, :depth], w_buf[slot], preferred_element_type=F32)
-        near_ref[i * half:(i + 1) * half, :] = prod[:half]
-        far_ref[i * half:(i + 1) * half, :] = prod[half:]
+        near_ref[i * half:(i + 1) * half, :] = prod[2 * i * half:(2 * i + 1) * half]
+        far_ref[i * half:(i + 1) * half, :] = prod[(2 * i + 1) * half:(2 * i + 2) * half]
 
     @pl.when(j + slots < tiles)
     def _():
@@ -169,6 +170,7 @@
     n_in = len(o_list)
     half = m_rows // 2
     tiles = count // COL_TILE
+    slots = min(W_SLOTS, tiles)
     out = jax.ShapeDtypeStruct((n_in * half, count), F32)
     raw = pl.BlockSpec(memory_space=pl.ANY)
     out_spec = pl.BlockSpec((n_in * half, COL_TILE), lambda j: (0, j))
@@ -179,10 +181,10 @@
         in_specs=[raw] * (n_in + 1),
         out_specs=(out_spec, out_spec),
         scratch_shapes=[
-            pltpu.VMEM((n_in, m_rows, depth + 128), BF16),
-            pltpu.VMEM((W_SLOTS, depth, COL_TILE), BF16),
+            pltpu.VMEM((n_in * m_rows, depth), BF16),
+            pltpu.VMEM((slots, depth, COL_TILE), BF16),
             pltpu.SemaphoreType.DMA((n_in,)),
-            pltpu.SemaphoreType.DMA((W_SLOTS,)),
+            pltpu.SemaphoreType.DMA((slots,)),
         ],
         compiler_params=pltpu.CompilerParams(dimension_semantics=("arbitrary",)),
         cost_estimate=pl.CostEstimate(flops=2 * n_in * m_rows * depth * count, bytes_accessed=depth * count * 2 + n_in * m_rows * count * 4, transcendentals=0),
@@ -290,45 +292,46 @@
         def after(value, *deps):
             return lax.optimization_barrier((value,) + deps)[0]
 
-        width = model_dim // COL_CHUNKS
-        arrived = [[None] * COL_CHUNKS for _ in range(n_seq)]
+        def tokens(rel):
+            return jnp.concatenate([q_rel[b][k] for b in range(n_seq) for k in (rel, rel + 1)], axis=0)
+
+        arrived = []
         pending = []
 
         def send_one():
-            b, j, near_part, came = pending.pop(0)
+            near_part, came = pending.pop(0)
             summed = near_part + came
-            arrived[b][j] = other_chip(summed)
+            arrived.append(other_chip(summed))
             return summed
 
-        near_part = None
+        q_far = queries(tokens(2))
+        o_far = []
         for b in range(n_seq):
-            q_lat = jnp.concatenate(q_rel[b][2:], axis=0)
-            if near_part is not None:
-                q_lat = after(q_lat, near_part)
-            q = queries(q_lat)
-            if pending:
-                q = after(q, send_one())
-            o = attend(2, b, q, 0)
-            for j in range(COL_CHUNKS):
-                if len(pending) > 1 - (j == 0):
-                    o = after(o, send_one())
-                near_part, far_part = out_proj([o], w_out, j * width, width)
-                pending.append((b, j, near_part, partner(far_part)))
-        q_lat = jnp.concatenate([q_rel[b][k] for b in range(n_seq) for k in (0, 1)], axis=0)
-        q_own = queries(after(q_lat, near_part))
+            o_far.append(attend(2, b, after(q_far, *o_far), b))
+        first = 0
+        for j, width in enumerate(FAR_WIDTHS):
+            deps = (send_one(),) if len(pending) > 1 else ()
+            if j:
+                deps += (near_part,)
+            near_part, far_part = out_proj([after(o_far[0], *deps), o_far[1]], w_out, first, width)
+            pending.append((near_part, partner(far_part)))
+            first += width
+        q_own = queries(after(tokens(0), near_part))
         dep = (send_one(),)
         o_own = []
         for b in range(n_seq):
             o_own.append(attend(0, b, after(q_own, *dep), b))
             dep = (o_own[-1],) + ((send_one(),) if pending else ())
-        cols = []
         flat = hidden.reshape(n_seq * n_tok, model_dim)
-        for j in range(COL_CHUNKS):
-            own_part, partner_part = out_proj([after(o_own[0], *dep), o_own[1]], w_out, j * width, width)
+        base = []
+        first = 0
+        for width in OWN_WIDTHS:
+            own_part, partner_part = out_proj([after(o_own[0], *dep), o_own[1]], w_out, first, width)
             dep = (own_part,)
-            base = own_part + partner(partner_part) + flat[:, j * width:(j + 1) * width].astype(F32)
-            cols.append(base + jnp.concatenate([arrived[b][j] for b in range(n_seq)], axis=0))
-        out = jnp.concatenate(cols, axis=1).astype(BF16).reshape(hidden.shape)
+            base.append(own_part + partner(partner_part))
+            first += width
+        total = jnp.concatenate(base, axis=1) + flat.astype(F32) + jnp.concatenate(arrived, axis=1)
+        out = total.astype(BF16).reshape(hidden.shape)
         lat_all, pe_all_t = write_caches(lengths, cache_lat, lat_new, cache_pe.transpose(0, 2, 1), pe_new.transpose(0, 2, 1))
         pe_all = pe_all_t.transpose(0, 2, 1)
         return out, lat_all, pe_all

time: 479 us -> 495 us (1.033)
  waiting for transfers between devices: 110 us -> 149 us
  matrix products: 106 us -> 99.2 us
  Pallas kernels: 195 us -> 189 us
  other arithmetic: 40.4 us -> 35.4 us
    ppermute x7 -> x6, waiting for transfers between devices: 110 us -> 145 us  [other_chip(): return lax.ppermute(value, 'tp', to_chip)]
    another operation x2 -> x1, other arithmetic: 9.66 us -> 0.8 us
    pallas_call x6 -> x5, Pallas kernels: 107 us -> 99.2 us  [out_proj(): pl.pallas_call(functools.partial(out_proj_kernel, n_in=n_in, first=first...]
    unnamed x3 -> x2, matrix products: 40.3 us -> 33.9 us
    add x0 -> x2, other arithmetic: none -> 5.47 us  [step(): base.append(own_part + partner(partner_part))]
    ppermute x7 -> x6, starting transfers between devices: 11.2 us -> 7.41 us  [other_chip(): return lax.ppermute(value, 'tp', to_chip)]
    add x4 -> x3, other arithmetic: 10.9 us -> 9.04 us  [send_one(): summed = near_part + came]
  transfers between devices with their start and end apart: 19 -> 17, of which waited for: 3 -> 4; matrix products, arithmetic and copies ran while one was open for 25% -> 21% of each run, Pallas kernels for 38% -> 18%
where the time goes in v3:
time: 495 us; the launch traced here: 490 us
  Pallas kernels  189 us (38%)
  waiting for transfers between devices  149 us (30%)
  matrix products  99.2 us (20%)
  other arithmetic  35.4 us (7%)
  starting transfers between devices  9.74 us (2%)
  local copies, waits for them, and re-layouts  6.55 us (1%)
    ppermute x6, waiting for transfers between devices, other_chip(): return lax.ppermute(value, 'tp', to_chip)  145 us
    pallas_call x5, Pallas kernels, out_proj(): pl.pallas_call(functools.partial(out_proj_kernel, n_in=n_in, first=first...  99.2 us
    pallas_call x4, Pallas kernels, attention(): pl.pallas_call(functools.partial(attention_kernel, scale=scale), out_shap...  83.5 us
    unnamed x2, matrix products  33.9 us
    dot_general x4, matrix products, project(): jnp.einsum('chv,sc->hvs', w_uv, lat, preferred_element_type=F32)  26.1 us
    dot_general x4, matrix products, project(): jnp.einsum('sc,chd->hsd', lat, w_uk, preferred_element_type=F32)  21.2 us
    dot_general x1, matrix products, step(): jnp.dot(normed, w_dq, preferred_element_type=F32)  11.9 us
  transfers between devices with their start and end apart: 17, of which 4 were waited for; matrix products, arithmetic and copies ran while one was open for 21% of the time, Pallas kernels for 18%

profile of v3, /device:TPU:0, one launch (start us, length us, event | category | flops | bytes accessed | tf_op | source)
XLA Modules:
  0.0 489.6 jit_solution(1540163749046778569)
XLA Ops:
  0.6 3.0 fusion.2
  3.8 1.8 fusion.4
  5.6 6.1 %fusion = f32[2,128,576]{1,2,0:T(8,128)S(1)} fusion(bf16[2,128,7168]{2,1,0:T(8,128)(2,1)S(1)} %fusion.4, bf16[7168,576]{0,1:T(8,128)(2,1)} %param.24), kind=kOutput, calls=%fused_computation.3 | convolution fusion | flops 2113929216 | bytes 12517376 | tf_op jit(solution)/shard_map/dot_general | solution.py:246
  12.0 0.8 subtract_convert_fusion
  12.8 0.8 fusion.51
  13.6 3.3 collective-permute-start.7
  16.9 11.9 %multiply_reduce_fusion = (f32[256]{0:T(256)S(1)}, f32[256,1536]{1,0:T(8,128)S(1)}) fusion(bf16[256,7168]{1,0:T(8,128)(2,1)} %bitcast.143, bf16[7168,1536]{1,0:T(8,128)(2,1)} %param.22), kind=kOutput, calls=%fused_computation.44 | convolution fusion | flops 5637931008 | bytes 27264000 | tf_op jit(solution)/shard_map/dot_general | solution.py:252
  29.1 2.0 collective-permute-start.4
  31.1 0.9 fusion.53
  32.0 0.9 fusion.54
  33.2 8.0 %convert_bitcast_fusion.5.v_old_ref = bf16[32,128,512]{2,1,0:T(8,128)(2,1)} fusion(bf16[512,32,128]{2,1,0:T(8,128)(2,1)} %param.28, bf16[2,512,512]{2,1,0:T(8,128)(2,1)S(1)} %slice_select_fusion), kind=kOutput, calls=%fused_computation.15 | convolution fusion | flops 2149580800 | bytes 8912896 | tf_op jit(solution)/shard_map/chv,sc->hvs/dot_general | solution.py:267
  41.3 6.0 %convert_bitcast_fusion.1.v_old_ref = bf16[32,128,512]{2,1,0:T(8,128)(2,1)} fusion(bf16[512,32,128]{2,1,0:T(8,128)(2,1)S(1)} %copy-done.20, bf16[2,512,512]{2,1,0:T(8,128)(2,1)S(1)} %slice_select_fusion), kind=kOutput, calls=%fused_computation.11 | convolution fusion | flops 2149580800 | bytes 8912896 | tf_op jit(solution)/shard_map/chv,sc->hvs/dot_general | solution.py:267
  47.2 4.6 convert_bitcast_fusion.7.k_old_ref
  51.8 4.7 convert_bitcast_fusion.3.k_old_ref
  56.5 0.6 dynamic-slice_bitcast_fusion.9
  57.2 0.6 maximum_bitcast_fusion.cos_ref
  59.6 0.6 pad_add_fusion.1.scal_ref
  61.4 1.2 pad_maximum_fusion.1
  62.9 6.0 %convert_bitcast_fusion.4.v_new_ref = bf16[32,128,512]{2,1,0:T(8,128)(2,1)} fusion(bf16[512,32,128]{2,1,0:T(8,128)(2,1)S(1)} %copy-done.21, bf16[2,512,576]{1,2,0:T(8,128)(2,1)S(1)} %pad_maximum_fusion.2), kind=kOutput, calls=%fused_computation.14 | convolution fusion | flops 2149580800 | bytes 8912896 | tf_op jit(solution)/shard_map/chv,sc->hvs/dot_general | solution.py:267
  69.0 4.9 convert_bitcast_fusion.6.k_new_ref
  73.8 6.0 %convert_bitcast_fusion.v_new_ref = bf16[32,128,512]{2,1,0:T(8,128)(2,1)} fusion(bf16[512,32,128]{2,1,0:T(8,128)(2,1)S(1)} %copy-done.21, bf16[2,512,576]{1,2,0:T(8,128)(2,1)S(1)} %pad_maximum_fusion.2), kind=kOutput, calls=%fused_computation.10 | convolution fusion | flops 2149580800 | bytes 8912896 | tf_op jit(solution)/shard_map/chv,sc->hvs/dot_general | solution.py:267
  80.1 0.8 copy.26.r_ref
  80.9 0.8 copy.35.r_ref
  81.7 7.1 %convert_bitcast_fusion.2.k_new_ref = bf16[32,512,128]{2,1,0:T(8,128)(2,1)} fusion(bf16[512,32,128]{2,1,0:T(8,128)(2,1)} %param.27, bf16[2,512,576]{1,2,0:T(8,128)(2,1)S(1)} %pad_maximum_fusion.2), kind=kOutput, calls=%fused_computation.12 | convolution fusion | flops 2149580800 | bytes 8912896 | tf_op jit(solution)/shard_map/sc,chd->hsd/dot_general | solution.py:266
  88.8 17.0 %fusion.39 = f32[512,6144]{0,1} fusion(bf16[1536,6144]{0,1:T(8,128)(2,1)} %bitcast.147, bf16[128,1536]{1,0:T(8,128)(2,1)} %collective-permute-done.5, bf16[128,1536]{1,0:T(8,128)(2,1)} %collective-permute-done.4, bf16[128,1536]{1,0:T(8,128)(2,1)} %collective-permute-done.3, bf16[128,1536]{1,0:T(8,128)(2,1)} %collective-permute-done.2), kind=kOutput, calls=%fused_computation.35 | convolution fusion | flops 9669967872 | bytes 33030144
  105.8 21.1 %attention.4.refs_0_ = bf16[256,4096]{1,0:T(8,128)(2,1)} custom-call(s32[3]{0:T(128)} %pad_add_fusion.1.scal_ref, f32[32,192,512]{2,1,0:T(8,128)} %bitcast.139, bf16[32,512,128]{2,1,0:T(8,128)(2,1)} %convert_bitcast_fusion.7.k_old_ref, bf16[32,512,128]{2,1,0:T(8,128)(2,1)} %convert_bitcast_fusion.6.k_new_ref, ...), custom_call_target="tpu_custom_call" | custom-call | flops 6442450944 | bytes 30000000 | tf_op jit(solution)/shard_map/attention/pallas_call | solution.py:108
  126.9 21.7 %attention.5.refs_1_ = bf16[256,4096]{1,0:T(8,128)(2,1)} custom-call(s32[3]{0:T(128)} %pad_add_fusion.1.scal_ref, f32[32,192,512]{2,1,0:T(8,128)} %bitcast.140, bf16[32,512,128]{2,1,0:T(8,128)(2,1)} %convert_bitcast_fusion.3.k_old_ref, bf16[32,512,128]{2,1,0:T(8,128)(2,1)} %convert_bitcast_fusion.2.k_new_ref, ...), custom_call_target="tpu_custom_call" | custom-call | flops 6442450944 | bytes 30000000 | tf_op jit(solution)/shard_map/attention/pallas_call | solution.py:108
  148.7 12.8 %out_proj.5 = (f32[256,1536]{1,0:T(8,128)}, f32[256,1536]{1,0:T(8,128)}) custom-call(bf16[256,4096]{1,0:T(8,128)(2,1)} %attention.4.refs_0_, bf16[256,4096]{1,0:T(8,128)(2,1)} %attention.5.refs_1_, bf16[4096,7168]{1,0:T(8,128)(2,1)} %refs_2_.9), custom_call_target="tpu_custom_call" | custom-call | flops 6442450944 | bytes 15728640 | tf_op jit(solution)/shard_map/out_proj/pallas_call | solution.py:177
  161.7 18.7 %out_proj.6 = (f32[256,2560]{1,0:T(8,128)}, f32[256,2560]{1,0:T(8,128)}) custom-call(bf16[256,4096]{1,0:T(8,128)(2,1)} %attention.4.refs_0_, bf16[256,4096]{1,0:T(8,128)(2,1)} %attention.5.refs_1_, bf16[4096,7168]{1,0:T(8,128)(2,1)} %refs_2_.9), custom_call_target="tpu_custom_call" | custom-call | flops 10737418240 | bytes 26214400 | tf_op jit(solution)/shard_map/out_proj/pallas_call | solution.py:177
  180.7 3.2 add.108
  184.0 21.0 %out_proj.7 = (f32[256,3072]{1,0:T(8,128)}, f32[256,3072]{1,0:T(8,128)}) custom-call(bf16[256,4096]{1,0:T(8,128)(2,1)} %attention.4.refs_0_, bf16[256,4096]{1,0:T(8,128)(2,1)} %attention.5.refs_1_, bf16[4096,7168]{1,0:T(8,128)(2,1)} %refs_2_.9), custom_call_target="tpu_custom_call" | custom-call | flops 12884901888 | bytes 31457280 | tf_op jit(solution)/shard_map/out_proj/pallas_call | solution.py:177
  208.7 2.9 collective-permute-done
  212.1 1.2 pad_maximum_fusion
  213.4 17.0 %fusion.55 = f32[512,6144]{0,1} fusion(bf16[512,1536]{1,0:T(8,128)(2,1)S(1)} %pad_maximum_fusion, bf16[1536,6144]{0,1:T(8,128)(2,1)} %bitcast.148), kind=kOutput, calls=%fused_computation.105 | convolution fusion | flops 9663676416 | bytes 33030144
  230.3 1.9 add.109
  232.3 20.3 %attention.6.refs_0_ = bf16[256,4096]{1,0:T(8,128)(2,1)} custom-call(s32[3]{0:T(128)} %pad_add_fusion.scal_ref, f32[32,192,512]{2,1,0:T(8,128)} %bitcast.137, bf16[32,512,128]{2,1,0:T(8,128)(2,1)} %convert_bitcast_fusion.7.k_old_ref, bf16[32,512,128]{2,1,0:T(8,128)(2,1)} %convert_bitcast_fusion.6.k_new_ref, ...), custom_call_target="tpu_custom_call" | custom-call | flops 6442450944 | bytes 30000000 | tf_op jit(solution)/shard_map/attention/pallas_call | solution.py:108
  252.5 3.9 add.111
  256.4 20.4 %attention.7.refs_1_ = bf16[256,4096]{1,0:T(8,128)(2,1)} custom-call(s32[3]{0:T(128)} %pad_add_fusion.scal_ref, f32[32,192,512]{2,1,0:T(8,128)} %bitcast.138, bf16[32,512,128]{2,1,0:T(8,128)(2,1)} %convert_bitcast_fusion.3.k_old_ref, bf16[32,512,128]{2,1,0:T(8,128)(2,1)} %convert_bitcast_fusion.2.k_new_ref, ...), custom_call_target="tpu_custom_call" | custom-call | flops 6442450944 | bytes 30000000 | tf_op jit(solution)/shard_map/attention/pallas_call | solution.py:108
  276.8 25.6 %out_proj.8 = (f32[256,4096]{1,0:T(8,128)}, f32[256,4096]{1,0:T(8,128)}) custom-call(bf16[256,4096]{1,0:T(8,128)(2,1)} %attention.6.refs_0_, bf16[256,4096]{1,0:T(8,128)(2,1)} %attention.7.refs_1_, bf16[4096,7168]{1,0:T(8,128)(2,1)} %refs_2_.9), custom_call_target="tpu_custom_call" | custom-call | flops 17179869184 | bytes 41943040 | tf_op jit(solution)/shard_map/out_proj/pallas_call | solution.py:177
  302.6 21.0 %out_proj.9 = (f32[256,3072]{1,0:T(8,128)}, f32[256,3072]{1,0:T(8,128)}) custom-call(bf16[256,4096]{1,0:T(8,128)(2,1)} %attention.6.refs_0_, bf16[256,4096]{1,0:T(8,128)(2,1)} %attention.7.refs_1_, bf16[4096,7168]{1,0:T(8,128)(2,1)} %refs_2_.9), custom_call_target="tpu_custom_call" | custom-call | flops 12884901888 | bytes 31457280 | tf_op jit(solution)/shard_map/out_proj/pallas_call | solution.py:177
  324.1 2.0 collective-permute-start.15
  326.1 1.3 copy.38.lat_new_ref
  327.4 6.1 %write_caches.1 = (bf16[2,1024,512]{2,1,0:T(8,128)(2,1)}, bf16[2,64,1024]{2,1,0:T(8,128)(2,1)}) custom-call(s32[2]{0:T(128)} %len_ref.1, bf16[2,1024,512]{2,1,0:T(8,128)(2,1)} %lat_ref.1, bf16[2,512,512]{2,1,0:T(8,128)(2,1)} %copy.38.lat_new_ref, bf16[2,64,1024]{2,1,0:T(8,128)(2,1)} %bitcast.145, bf16[2,64,512]{2,1,0:T(8,128)(2,1)} %bitcast.144), custom_call_target="tpu_custom_call" | custom-call | flops 20000000 | bytes 4194304 | tf_op jit(solution)/shard_map/write_caches/pallas_call | solution.py:209
  333.5 2.4 add.113
  335.9 0.7 copy-done.4
  336.6 3.1 add.112
  339.7 144.7 %collective-permute-done.14 = f32[256,1536]{1,0:T(8,128)} collective-permute-done((f32[256,1536]{1,0:T(8,128)}, f32[256,1536]{1,0:T(8,128)}, u32[]{:S(2)}, u32[]{:S(2)}) %collective-permute-start.14) | collective-permute-done | bytes 1572896 | tf_op jit(solution)/shard_map/ppermute | solution.py:233
  484.4 4.9 %fusion.6 = bf16[2,128,7168]{2,1,0:T(8,128)(2,1)} fusion(bf16[2,128,7168]{2,1,0:T(8,128)(2,1)S(1)} %copy-done.1, f32[2,128,3072]{2,1,0:T(8,128)S(1)} %bitcast.142, f32[2,128,4096]{2,1,0:T(8,128)S(1)} %bitcast.141, f32[2,128,3072]{2,1,0:T(8,128)} %bitcast.72, f32[2,128,2560]{2,1,0:T(8,128)} %bitcast.71, f32[2,128,1536]{2,1,0:T(8,128)} %bitcast.70), kind=kLoop, calls=%fused_computation.9 | loop fusion | flops 12845056 | bytes 22020096 | tf_op jit(solution)/shard_map/convert_element_type | solution.py:334
  (104 shorter events, 9.9 us)
Async XLA Ops:
  0.6 3.1 copy-start
  5.6 6.2 %copy-start.5 = (bf16[2,128,7168]{2,1,0:T(8,128)(2,1)}, bf16[2,128,7168]{2,1,0:T(8,128)(2,1)S(1)}, u32[]{:S(2)}) copy-start(bf16[2,128,7168]{2,1,0:T(8,128)(2,1)S(1)} %fusion.4) | copy-start | bytes 11010052
  5.6 6.3 %copy-start.19 = (f32[512]{0:T(512)S(1)}, f32[512]{0:T(512)}, u32[]{:S(2)}) copy-start(f32[512]{0:T(512)} %param.25) | copy-start | bytes 6148
  13.6 46.0 %collective-permute-start.7 = (bf16[2,128,576]{1,2,0:T(8,128)(2,1)}, bf16[2,128,576]{1,2,0:T(8,128)(2,1)}, u32[]{:S(2)}, u32[]{:S(2)}) collective-permute-start(bf16[2,128,576]{1,2,0:T(8,128)(2,1)} %get-tuple-element.54), channel_id=1, source_target_pairs={{0,2},{1,3},{2,0},{3,1},{4,6},{5,7},{6,4},{7,5}} | collective-permute-start | bytes 884744 | tf_op jit(solution)/shard_map/ppermute | solution.py:233
  16.9 44.0 %collective-permute-start.6 = (bf16[2,128,576]{1,2,0:T(8,128)(2,1)}, bf16[2,128,576]{1,2,0:T(8,128)(2,1)}, u32[]{:S(2)}, u32[]{:S(2)}) collective-permute-start(bf16[2,128,576]{1,2,0:T(8,128)(2,1)} %get-tuple-element.54), channel_id=1, source_target_pairs={{0,1},{1,0},{2,3},{3,2},{4,5},{5,4},{6,7},{7,6}} | collective-permute-start | bytes 884744 | tf_op jit(solution)/shard_map/ppermute | solution.py:230
  16.9 11.9 %copy-start.16 = (f32[1536]{0:T(1024)S(1)}, f32[1536]{0:T(1024)}, u32[]{:S(2)}) copy-start(f32[1536]{0:T(1024)} %param.23) | copy-start | bytes 18436
  28.8 4.1 copy-start.17
  28.8 4.2 copy-start.2
  29.1 31.2 %collective-permute-start.2 = (bf16[128,1536]{1,0:T(8,128)(2,1)S(1)}, bf16[128,1536]{1,0:T(8,128)(2,1)}, u32[]{:S(2)}, u32[]{:S(2)}) collective-permute-start(bf16[128,1536]{1,0:T(8,128)(2,1)S(1)} %get-tuple-element.49), channel_id=1, source_target_pairs={{0,2},{1,3},{2,0},{3,1},{4,6},{5,7},{6,4},{7,5}} | collective-permute-start | bytes 1179656 | tf_op jit(solution)/shard_map/ppermute | solution.py:233
  29.1 31.7 %collective-permute-start.4 = (bf16[128,1536]{1,0:T(8,128)(2,1)S(1)}, bf16[128,1536]{1,0:T(8,128)(2,1)}, u32[]{:S(2)}, u32[]{:S(2)}) collective-permute-start(bf16[128,1536]{1,0:T(8,128)(2,1)S(1)} %get-tuple-element.50), channel_id=1, source_target_pairs={{0,2},{1,3},{2,0},{3,1},{4,6},{5,7},{6,4},{7,5}} | collective-permute-start | bytes 1179656 | tf_op jit(solution)/shard_map/ppermute | solution.py:233
  33.0 8.2 %copy-start.14 = (pred[2,512]{1,0:T(4,128)(4,1)}, pred[2,512]{1,0:T(4,128)(4,1)S(1)}, u32[]{:S(2)}) copy-start(pred[2,512]{1,0:T(4,128)(4,1)S(1)} %iota_compare_fusion.1) | copy-start | bytes 3076
  33.2 8.0 %copy-start.20 = (bf16[512,32,128]{2,1,0:T(8,128)(2,1)S(1)}, bf16[512,32,128]{2,1,0:T(8,128)(2,1)}, u32[]{:S(2)}) copy-start(bf16[512,32,128]{2,1,0:T(8,128)(2,1)} %param.28) | copy-start | bytes 12582916
  41.3 6.0 %copy-start.22 = (bf16[512,32,128]{2,1,0:T(8,128)(2,1)S(1)}, bf16[512,32,128]{2,1,0:T(8,128)(2,1)}, u32[]{:S(2)}) copy-start(bf16[512,32,128]{2,1,0:T(8,128)(2,1)} %param.27) | copy-start | bytes 12582916
  51.8 8.5 %copy-start.18 = (s32[2]{0:T(128)S(1)}, s32[2]{0:T(128)}, u32[]{:S(2)}) copy-start(s32[2]{0:T(128)} %len_ref.1) | copy-start | bytes 28
  57.8 5.1 %copy-start.21 = (bf16[512,32,128]{2,1,0:T(8,128)(2,1)S(1)}, bf16[512,32,128]{2,1,0:T(8,128)(2,1)}, u32[]{:S(2)}) copy-start(bf16[512,32,128]{2,1,0:T(8,128)(2,1)} %param.28) | copy-start | bytes 12582916
  59.6 1.8 collective-permute-start.8
  60.3 28.5 %collective-permute-start.3 = (bf16[128,1536]{1,0:T(8,128)(2,1)}, bf16[128,1536]{1,0:T(8,128)(2,1)}, u32[]{:S(2)}, u32[]{:S(2)}) collective-permute-start(bf16[128,1536]{1,0:T(8,128)(2,1)} %collective-permute-done.2), channel_id=1, source_target_pairs={{0,1},{1,0},{2,3},{3,2},{4,5},{5,4},{6,7},{7,6}} | collective-permute-start | bytes 1179656 | tf_op jit(solution)/shard_map/ppermute | solution.py:230
  60.9 28.0 %collective-permute-start.5 = (bf16[128,1536]{1,0:T(8,128)(2,1)}, bf16[128,1536]{1,0:T(8,128)(2,1)}, u32[]{:S(2)}, u32[]{:S(2)}) collective-permute-start(bf16[128,1536]{1,0:T(8,128)(2,1)} %collective-permute-done.4), channel_id=1, source_target_pairs={{0,1},{1,0},{2,3},{3,2},{4,5},{5,4},{6,7},{7,6}} | collective-permute-start | bytes 1179656 | tf_op jit(solution)/shard_map/ppermute | solution.py:230
  62.9 18.9 %copy-start.3 = (bf16[2,512,576]{1,2,0:T(8,128)(2,1)}, bf16[2,512,576]{1,2,0:T(8,128)(2,1)S(1)}, u32[]{:S(2)}) copy-start(bf16[2,512,576]{1,2,0:T(8,128)(2,1)S(1)} %pad_maximum_fusion.2) | copy-start | bytes 3538948
  62.9 6.1 %copy-start.23 = (bf16[512,32,128]{2,1,0:T(8,128)(2,1)S(1)}, bf16[512,32,128]{2,1,0:T(8,128)(2,1)}, u32[]{:S(2)}) copy-start(bf16[512,32,128]{2,1,0:T(8,128)(2,1)} %param.27) | copy-start | bytes 12582916
  73.8 6.0 %copy-start.10 = (bf16[2,1024,64]{1,2,0:T(8,128)(2,1)S(1)}, bf16[2,1024,64]{1,2,0:T(8,128)(2,1)}, u32[]{:S(2)}) copy-start(bf16[2,1024,64]{1,2,0:T(8,128)(2,1)} %param.20) | copy-start | bytes 786436
  73.8 6.0 %copy-start.15 = (pred[2,512]{1,0:T(4,128)(4,1)S(1)}, pred[2,512]{1,0:T(4,128)(4,1)}, u32[]{:S(2)}) copy-start(pred[2,512]{1,0:T(4,128)(4,1)} %copy-done.14) | copy-start | bytes 3076
  79.9 8.9 %copy-start.9 = (bf16[2,512,64]{1,2,0:T(8,128)(2,1)}, bf16[2,512,64]{1,2,0:T(8,128)(2,1)S(1)}, u32[]{:S(2)}) copy-start(bf16[2,512,64]{1,2,0:T(8,128)(2,1)S(1)} %get-tuple-element.85) | copy-start | bytes 393220
  161.5 19.2 %collective-permute-start.9 = (f32[256,1536]{1,0:T(8,128)}, f32[256,1536]{1,0:T(8,128)}, u32[]{:S(2)}, u32[]{:S(2)}) collective-permute-start(f32[256,1536]{1,0:T(8,128)} %get-tuple-element.25), channel_id=1, source_target_pairs={{0,1},{1,0},{2,3},{3,2},{4,5},{5,4},{6,7},{7,6}} | collective-permute-start | bytes 4718600 | tf_op jit(solution)/shard_map/ppermute | solution.py:230
  180.3 50.0 %collective-permute-start.10 = (f32[256,2560]{1,0:T(8,128)}, f32[256,2560]{1,0:T(8,128)S(1)}, u32[]{:S(2)}, u32[]{:S(2)}) collective-permute-start(f32[256,2560]{1,0:T(8,128)} %get-tuple-element.31), channel_id=1, source_target_pairs={{0,1},{1,0},{2,3},{3,2},{4,5},{5,4},{6,7},{7,6}} | collective-permute-start | bytes 7864328 | tf_op jit(solution)/shard_map/ppermute | solution.py:230
  184.0 21.7 %copy-start.12 = (f32[128,32]{0,1:T(8,128)S(1)}, f32[128,32]{0,1:T(8,128)}, u32[]{:S(2)}) copy-start(f32[128,32]{0,1:T(8,128)} %get-tuple-element.83) | copy-start | bytes 49156
  184.0 21.7 %copy-start.13 = (f32[128,32]{0,1:T(8,128)S(1)}, f32[128,32]{0,1:T(8,128)}, u32[]{:S(2)}) copy-start(f32[128,32]{0,1:T(8,128)} %get-tuple-element.84) | copy-start | bytes 49156
  184.0 22.9 %copy-start.11 = (f32[128,32]{0,1:T(8,128)S(1)}, f32[128,32]{0,1:T(8,128)}, u32[]{:S(2)}) copy-start(f32[128,32]{0,1:T(8,128)} %get-tuple-element.68) | copy-start | bytes 49156
  205.0 47.5 %collective-permute-start.11 = (f32[256,3072]{1,0:T(8,128)}, f32[256,3072]{1,0:T(8,128)}, u32[]{:S(2)}, u32[]{:S(2)}) collective-permute-start(f32[256,3072]{1,0:T(8,128)} %get-tuple-element.33), channel_id=1, source_target_pairs={{0,1},{1,0},{2,3},{3,2},{4,5},{5,4},{6,7},{7,6}} | collective-permute-start | bytes 9437192 | tf_op jit(solution)/shard_map/ppermute | solution.py:230
  205.1 6.4 %collective-permute-start = (bf16[128,1536]{1,0:T(8,128)(2,1)S(1)}, bf16[128,1536]{1,0:T(8,128)(2,1)}, u32[]{:S(2)}, u32[]{:S(2)}) collective-permute-start(bf16[128,1536]{1,0:T(8,128)(2,1)S(1)} %get-tuple-element.49), channel_id=1, source_target_pairs={{0,1},{1,0},{2,3},{3,2},{4,5},{5,4},{6,7},{7,6}} | collective-permute-start | bytes 1179656 | tf_op jit(solution)/shard_map/ppermute | solution.py:230
  205.5 6.6 %collective-permute-start.1 = (bf16[128,1536]{1,0:T(8,128)(2,1)S(1)}, bf16[128,1536]{1,0:T(8,128)(2,1)}, u32[]{:S(2)}, u32[]{:S(2)}) collective-permute-start(bf16[128,1536]{1,0:T(8,128)(2,1)S(1)} %get-tuple-element.50), channel_id=1, source_target_pairs={{0,1},{1,0},{2,3},{3,2},{4,5},{5,4},{6,7},{7,6}} | collective-permute-start | bytes 1179656 | tf_op jit(solution)/shard_map/ppermute | solution.py:230
  213.4 17.0 %copy-start.8 = (f32[256,2560]{1,0:T(8,128)S(1)}, f32[256,2560]{1,0:T(8,128)}, u32[]{:S(2)}) copy-start(f32[256,2560]{1,0:T(8,128)} %get-tuple-element.27) | copy-start | bytes 7864324
  232.3 20.3 %copy-start.6 = (f32[256,3072]{1,0:T(8,128)S(1)}, f32[256,3072]{1,0:T(8,128)}, u32[]{:S(2)}) copy-start(f32[256,3072]{1,0:T(8,128)} %get-tuple-element.29) | copy-start | bytes 9437188
  302.4 33.5 %collective-permute-start.12 = (f32[256,4096]{1,0:T(8,128)}, f32[256,4096]{1,0:T(8,128)}, u32[]{:S(2)}, u32[]{:S(2)}) collective-permute-start(f32[256,4096]{1,0:T(8,128)} %get-tuple-element.37), channel_id=1, source_target_pairs={{0,1},{1,0},{2,3},{3,2},{4,5},{5,4},{6,7},{7,6}} | collective-permute-start | bytes 12582920 | tf_op jit(solution)/shard_map/ppermute | solution.py:230
  302.6 23.5 %slice-start = ((bf16[2,512,576]{1,2,0:T(8,128)(2,1)}), bf16[2,512,512]{1,2,0:T(8,128)(2,1)S(1)}, s32[]{:S(2)}) async-start(bf16[2,512,576]{1,2,0:T(8,128)(2,1)} %copy-done.3), calls=%async_computation | async-start | bytes 2097152 | tf_op jit(solution)/shard_map/slice | solution.py:261
  323.7 9.8 %collective-permute-start.13 = (f32[256,3072]{1,0:T(8,128)}, f32[256,3072]{1,0:T(8,128)}, u32[]{:S(2)}, u32[]{:S(2)}) collective-permute-start(f32[256,3072]{1,0:T(8,128)} %get-tuple-element.40), channel_id=1, source_target_pairs={{0,1},{1,0},{2,3},{3,2},{4,5},{5,4},{6,7},{7,6}} | collective-permute-start | bytes 9437192 | tf_op jit(solution)/shard_map/ppermute | solution.py:230
  324.0 160.4 %collective-permute-start.16 = (f32[256,3072]{1,0:T(8,128)}, f32[256,3072]{1,0:T(8,128)}, u32[]{:S(2)}, u32[]{:S(2)}) collective-permute-start(f32[256,3072]{1,0:T(8,128)} %add.111), channel_id=1, source_target_pairs={{0,2},{1,3},{2,0},{3,1},{4,6},{5,7},{6,4},{7,5}} | collective-permute-start | bytes 9437192 | tf_op jit(solution)/shard_map/ppermute | solution.py:233
  324.1 160.3 %collective-permute-start.15 = (f32[256,2560]{1,0:T(8,128)}, f32[256,2560]{1,0:T(8,128)}, u32[]{:S(2)}, u32[]{:S(2)}) collective-permute-start(f32[256,2560]{1,0:T(8,128)} %add.109), channel_id=1, source_target_pairs={{0,2},{1,3},{2,0},{3,1},{4,6},{5,7},{6,4},{7,5}} | collective-permute-start | bytes 7864328 | tf_op jit(solution)/shard_map/ppermute | solution.py:233
  326.1 158.3 %collective-permute-start.14 = (f32[256,1536]{1,0:T(8,128)}, f32[256,1536]{1,0:T(8,128)}, u32[]{:S(2)}, u32[]{:S(2)}) collective-permute-start(f32[256,1536]{1,0:T(8,128)} %add.108), channel_id=1, source_target_pairs={{0,2},{1,3},{2,0},{3,1},{4,6},{5,7},{6,4},{7,5}} | collective-permute-start | bytes 4718600 | tf_op jit(solution)/shard_map/ppermute | solution.py:233
  327.4 6.1 %copy-start.7 = (f32[256,3072]{1,0:T(8,128)S(1)}, f32[256,3072]{1,0:T(8,128)}, u32[]{:S(2)}) copy-start(f32[256,3072]{1,0:T(8,128)} %get-tuple-element.39) | copy-start | bytes 9437188
  333.5 3.1 copy-start.4
  335.9 148.5 %copy-start.1 = (bf16[2,128,7168]{2,1,0:T(8,128)(2,1)S(1)}, bf16[2,128,7168]{2,1,0:T(8,128)(2,1)}, u32[]{:S(2)}) copy-start(bf16[2,128,7168]{2,1,0:T(8,128)(2,1)} %param.15) | copy-start | bytes 11010052
